TPU v7x, 16 devices: a 4x2x1 block of a 4x4x8 slice. The times are simulated.
16 devices in a mesh: dp: 2 (over y, z), tp: 8 (over x, core).
Axes of the slice: x: 4, y: 2, z: 1, core: 2. Of those that a mesh axis runs over, the one named last changes fastest.
The devices are a block of a 4x4x8 slice.
Arguments:
- x: bfloat16 [4096, 2048], P('dp'), parts along dimension 0
- dy: bfloat16 [4096, 2048], P('dp'), parts along dimension 0
- gate: bfloat16 [4096, 5120], P('dp', 'tp'), parts along dimension 0
- up: bfloat16 [4096, 5120], P('dp', 'tp'), parts along dimension 0
- w_gate: bfloat16 [2048, 5120], P(None, 'tp')
- w_up: bfloat16 [2048, 5120], P(None, 'tp')
- w_down: bfloat16 [5120, 2048], P('tp')
Outputs:
- output 1: bfloat16 [4096, 2048], P('dp'), parts along dimension 0
- output 2: bfloat16 [4096, 5120], P('dp', 'tp'), parts along dimension 0
- output 3: bfloat16 [4096, 5120], P('dp', 'tp'), parts along dimension 0
- output 4: bfloat16 [10240, 2048], P(('dp', 'tp')), parts along dimension 0
There are 2 independent parts. A program takes and returns all parts, laid end to end along the dimension named above; an argument that names none is the same for every part.
All inputs are finite; a program needn't handle non-finite values.
Results may differ from a plain program's by a relative error of at most 0.012.
Values are sent between devices in bfloat16 or wider.
A program may use at most 768 MiB of HBM per device.

v0:
```python
import jax
import jax.numpy as jnp
from jax import lax
from jax.sharding import PartitionSpec as P


def act(gate, up):
    return jax.nn.gelu(gate) * up


def solution(mesh):
    def step(x, dy, gate, up, w_gate, w_up, w_down):
        hidden, back = jax.vjp(act, gate.astype(jnp.float32), up.astype(jnp.float32))
        d_hidden = jnp.dot(dy, w_down.T, preferred_element_type=jnp.float32)
        d_gate, d_up = (g.astype(jnp.bfloat16) for g in back(d_hidden))
        term = jnp.dot(d_gate, w_gate.T, preferred_element_type=jnp.float32) + jnp.dot(d_up, w_up.T, preferred_element_type=jnp.float32)
        dx = lax.psum(term.astype(jnp.bfloat16), "tp")
        dw_gate = jnp.dot(x.T, d_gate, preferred_element_type=jnp.float32)
        dw_up = jnp.dot(x.T, d_up, preferred_element_type=jnp.float32)
        dw_down = jnp.dot(hidden.astype(jnp.bfloat16).T, dy, preferred_element_type=jnp.float32)
        return dx, *(g.astype(jnp.bfloat16) for g in (dw_gate, dw_up, dw_down))

    tokens, columns, rows = P("dp", None), P(None, "tp"), P("tp", None)
    return jax.shard_map(
        step,
        mesh=mesh,
        in_specs=(tokens, tokens, P("dp", "tp"), P("dp", "tp"), columns, columns, rows),
        out_specs=(tokens, P("dp", "tp"), P("dp", "tp"), P(("dp", "tp"), None)),
        check_vma=False,
    )
```

profile of v0, /device:TPU:113, one launch (start us, length us, event | category | flops | bytes accessed | tf_op | source)
XLA Modules:
  0.0 162.1 jit_solution(9671938679312134032)
XLA Ops:
  7.2 0.0 copy-start
  7.2 0.1 all-reduce.2.cloned.1.call-start
  7.3 15.2 %fusion.4 = (bf16[2048,640]{1,0:T(8,128)(2,1)S(1)}, f32[2048,640]{1,0:T(8,128)}) fusion(bf16[2048,640]{1,0:T(8,128)(2,1)} %param.9, bf16[2048,640]{1,0:T(8,128)(2,1)} %param.10, bf16[2048,2048]{1,0:T(8,128)(2,1)} %param.8, bf16[640,2048]{1,0:T(8,128)(2,1)} %param.13), kind=kOutput, calls=%fused_computation.12 | convolution fusion | flops 5398855680 | bytes 24117248 | tf_op jit(solution)/shard_map/dot_general | solution.py:14
  22.5 0.0 copy-start.3
  22.5 0.0 copy-done
  22.5 0.0 copy-start.2
  22.5 9.6 %fusion.21 = f32[2048,2048]{1,0:T(8,128)} fusion(bf16[2048,640]{1,0:T(8,128)(2,1)S(1)} %get-tuple-element.8, bf16[2048,640]{1,0:T(8,128)(2,1)S(1)} %copy-done), kind=kOutput, calls=%fused_computation.32 | convolution fusion | flops 5368709120 | bytes 22020096 | tf_op jit(solution)/shard_map/dot_general | solution.py:16
  32.1 0.0 copy-done.3
  32.1 0.0 copy-done.2
  32.1 16.0 %add_convert_fusion = bf16[2048,2048]{1,0:T(8,128)(2,1)} fusion(f32[2048,2048]{1,0:T(8,128)} %fusion.21, bf16[2048,640]{1,0:T(8,128)(2,1)S(1)} %copy-done.2, f32[2048,640]{1,0:T(8,128)} %get-tuple-element.9, bf16[2048,640]{1,0:T(8,128)(2,1)} %param.9), kind=kOutput, calls=%fused_computation | convolution fusion | flops 5391515648 | bytes 35651584 | tf_op jit(solution)/shard_map/dot_general | solution.py:16
  48.1 0.1 all-reduce.2.cloned.1.call-update
  48.2 8.9 %fusion.10 = bf16[2048,640]{0,1:T(8,128)(2,1)S(1)} fusion(bf16[2048,640]{1,0:T(8,128)(2,1)} %copy-done.3, bf16[2048,2048]{1,0:T(8,128)(2,1)} %param.7), kind=kOutput, calls=%fused_computation.22 | convolution fusion | flops 5370019840 | bytes 13631488 | tf_op jit(solution)/shard_map/dot_general | solution.py:18
  57.1 2.8 %copy.11 = bf16[2048,640]{1,0:T(8,128)(2,1)} copy(bf16[2048,640]{0,1:T(8,128)(2,1)S(1)} %fusion.10) | data formatting | bytes 5242880
  59.8 11.7 %fusion.11 = bf16[2048,640]{0,1:T(8,128)(2,1)S(1)} fusion(bf16[2048,2048]{1,0:T(8,128)(2,1)} %param.7, f32[2048,640]{1,0:T(8,128)} %get-tuple-element.9, bf16[2048,640]{1,0:T(8,128)(2,1)} %param.9), kind=kOutput, calls=%fused_computation.23 | convolution fusion | flops 5384437760 | bytes 18874368 | tf_op jit(solution)/shard_map/dot_general | solution.py:19
  71.5 2.6 %copy.12 = bf16[2048,640]{1,0:T(8,128)(2,1)} copy(bf16[2048,640]{0,1:T(8,128)(2,1)S(1)} %fusion.11) | data formatting | bytes 5242880
  74.1 0.0 copy-start.1
  74.1 12.7 %convolution_convert_fusion = bf16[640,2048]{1,0:T(8,128)(2,1)} fusion(bf16[2048,2048]{1,0:T(8,128)(2,1)} %param.8, bf16[2048,640]{1,0:T(8,128)(2,1)} %param.10, bf16[2048,640]{1,0:T(8,128)(2,1)} %param.9), kind=kOutput, calls=%fused_computation.19 | convolution fusion | flops 5385748480 | bytes 16252928 | tf_op jit(solution)/shard_map/dot_general | solution.py:20
  86.8 60.0 %all-reduce.2.cloned.1.call-done = bf16[2048,2048]{1,0:T(8,128)(2,1)} async-done(((bf16[2048,2048]{1,0:T(8,128)(2,1)}), bf16[2048,2048]{1,0:T(8,128)(2,1)}) %all-reduce.2.cloned.1.call-update) | async-done | bytes 8388624 | tf_op jit(solution)/shard_map/psum | solution.py:17
  146.8 8.4 %copy.14 = bf16[2048,2048]{1,0:T(8,128)(2,1)} copy(bf16[2048,2048]{1,0:T(8,128)(2,1)} %all-reduce.2.cloned.1.call-done) | data formatting | bytes 16777216
  155.2 0.0 copy-done.1
Async XLA Ops:
  7.2 15.3 %copy-start = (bf16[2048,640]{1,0:T(8,128)(2,1)S(1)}, bf16[2048,640]{1,0:T(8,128)(2,1)}, u32[]{:S(2)}) copy-start(bf16[2048,640]{1,0:T(8,128)(2,1)} %param.11) | copy-start | bytes 7864324
  7.2 139.6 %all-reduce.2.cloned.1.call-start = ((), (), s32[]{:S(2)}) async-start(), calls=%async_computation | async-start | bytes 16777216 | tf_op jit(solution)/shard_map/psum | solution.py:17
  22.5 9.6 %copy-start.3 = (bf16[2048,640]{1,0:T(8,128)(2,1)}, bf16[2048,640]{1,0:T(8,128)(2,1)S(1)}, u32[]{:S(2)}) copy-start(bf16[2048,640]{1,0:T(8,128)(2,1)S(1)} %get-tuple-element.8) | copy-start | bytes 7864324
  22.5 9.6 %copy-start.2 = (bf16[2048,640]{1,0:T(8,128)(2,1)S(1)}, bf16[2048,640]{1,0:T(8,128)(2,1)}, u32[]{:S(2)}) copy-start(bf16[2048,640]{1,0:T(8,128)(2,1)} %param.12) | copy-start | bytes 7864324
  74.1 81.1 %copy-start.1 = (bf16[2048,640]{1,0:T(8,128)(2,1)S(1)}, bf16[2048,640]{1,0:T(8,128)(2,1)}, u32[]{:S(2)}) copy-start(bf16[2048,640]{1,0:T(8,128)(2,1)} %param.11) | copy-start | bytes 7864324
Sparse Core Ops, SparseCore 0:
  48.3 98.4 all-reduce.1
where the time goes:
time: 162 us
  matrix products  74.1 us (46%)
  waiting for transfers between devices  60.1 us (37%)
  between operations  14.1 us (9%)
  local copies, waits for them, and re-layouts  13.8 us (9%)
    psum x1, waiting for transfers between devices, step(): dx = lax.psum(term.astype(jnp.bfloat16), 'tp')  60 us
    dot_general x1, matrix products, step(): jnp.dot(d_up, w_up.T, preferred_element_type=jnp.float32)  16 us
    dot_general x1, matrix products, step(): d_hidden = jnp.dot(dy, w_down.T, preferred_element_type=jnp.float32)  15.2 us
    unnamed x11, local copies, waits for them, and re-layouts  13.8 us
    dot_general x1, matrix products, step(): jnp.dot(hidden.astype(jnp.bfloat16).T, dy, preferred_element_type=jnp.flo...  12.7 us
    dot_general x1, matrix products, step(): dw_up = jnp.dot(x.T, d_up, preferred_element_type=jnp.float32)  11.7 us
    dot_general x1, matrix products, step(): jnp.dot(d_gate, w_gate.T, preferred_element_type=jnp.float32)  9.59 us
    dot_general x1, matrix products, step(): dw_gate = jnp.dot(x.T, d_gate, preferred_element_type=jnp.float32)  8.89 us
  transfers between devices with their start and end apart: 1, of which 1 were waited for; matrix products, arithmetic and copies ran while one was open for 24% of the time, Pallas kernels for 0%

commit v1 on v0

v1 whole, which is shorter than its diff:
```python
import functools

import jax
import jax.numpy as jnp
from jax import lax
from jax.experimental import pallas as pl
from jax.experimental.pallas import tpu as pltpu
from jax.sharding import PartitionSpec as P

MESH = pl.DeviceIdType.MESH
CHIPS = 4
BLOCK = 256
PART = BLOCK // 2
STRIP = 32
TILE = 256


def act(gate, up):
    return jax.nn.gelu(gate) * up


def dot(a, b, contract):
    return lax.dot_general(a, b, ((contract[:1], contract[1:]), ((), ())), preferred_element_type=jnp.float32)


def main_kernel(
    x_hbm, dy_hbm, gate_hbm, up_hbm, wg_hbm, wu_hbm, wd_hbm,
    dx, dw, dwd,
    x, dy, gu, w, wd, hid, hid_t, dh, own, stage, sendbuf, far, near,
    in_sem, row_sem, term_send, term_recv, rs_send, far_recv, near_recv,
    ag_send, ag_recv, fwd_send, fwd_recv, peer_send, peer_recv,
):
    tokens, d = x.shape
    f = wd.shape[0]
    half = d // 2
    chunk_rows = tokens // CHIPS
    me = lax.axis_index("tp")
    chip, core = lax.div(me, 2), lax.rem(me, 2)
    peer = chip * 2 + 1 - core
    mine = pl.ds(pl.multiple_of(core * half, half), half)
    theirs = pl.ds(pl.multiple_of((1 - core) * half, half), half)

    def chip_at(step):
        return lax.rem(chip + step, CHIPS)

    def device_at(step):
        return chip_at(step) * 2 + core

    steps = (1, CHIPS - 1)

    barrier = pltpu.get_barrier_semaphore()
    for other in (device_at(1), device_at(CHIPS - 1), peer):
        pl.semaphore_signal(barrier, inc=1, device_id={"tp": other}, device_id_type=MESH)

    def remote(src, dst, send, recv, device):
        return pltpu.make_async_remote_copy(
            src_ref=src, dst_ref=dst, send_sem=send, recv_sem=recv, device_id={"tp": device}, device_id_type=MESH
        )

    def row_at(step, i, p=0):
        return pl.multiple_of(chip_at(step) * chunk_rows + i * BLOCK + p * PART, PART)

    def row_copies(b, step, i):
        r = pl.ds(row_at(step, i), BLOCK)
        return (
            pltpu.make_async_copy(dy_hbm.at[r], dy.at[r], row_sem.at[0, b]),
            pltpu.make_async_copy(gate_hbm.at[r], gu.at[r, pl.ds(0, f)], row_sem.at[1, b]),
            pltpu.make_async_copy(up_hbm.at[r], gu.at[r, pl.ds(f, f)], row_sem.at[2, b]),
        )

    def start_rows(b, step, i):
        for c in row_copies(b, step, i):
            c.start()

    def x_copy(b):
        r = pl.ds(pl.multiple_of(b * BLOCK, BLOCK), BLOCK)
        return pltpu.make_async_copy(x_hbm.at[r], x.at[r], row_sem.at[3, b])

    in_wd = pltpu.make_async_copy(wd_hbm, wd, in_sem.at[0])
    in_wg = pltpu.make_async_copy(wg_hbm, w.at[:, pl.ds(0, f)], in_sem.at[1])
    in_wu = pltpu.make_async_copy(wu_hbm, w.at[:, pl.ds(f, f)], in_sem.at[2])
    in_wd.start()
    start_rows(0, 2, 0)
    in_wg.start()
    in_wu.start()
    start_rows(1, 2, 1)

    def hidden_block(b, step, i):
        start = row_at(step, i)
        for c in row_copies(b, step, i):
            c.wait()
        dh[...] = dot(dy[pl.ds(start, BLOCK), :], wd[...], (1, 1))

        @pl.loop(0, BLOCK // STRIP)
        def _(s):
            here = pl.ds(pl.multiple_of(s * STRIP, STRIP), STRIP)
            r = pl.ds(pl.multiple_of(start + s * STRIP, STRIP), STRIP)
            h, back = jax.vjp(act, gu[r, pl.ds(0, f)].astype(jnp.float32), gu[r, pl.ds(f, f)].astype(jnp.float32))
            d_gate, d_up = back(dh[here, :])
            gu[r, pl.ds(0, f)] = d_gate.astype(gu.dtype)
            gu[r, pl.ds(f, f)] = d_up.astype(gu.dtype)
            hid[here, :] = h.astype(hid.dtype)

        hid_t[:, pl.ds(pl.multiple_of(start, BLOCK), BLOCK)] = hid[...].T

    def term_copy(b, step, i, slot):
        rows = pl.ds(row_at(step, i), BLOCK)
        return remote(stage.at[slot], dx.at[rows, theirs], term_send.at[slot], term_recv.at[b], peer)

    def term_block(b, step, i, slot):
        rows = pl.ds(row_at(step, i), BLOCK)
        width = half // 2
        for q in range(2):
            cols = pl.ds(pl.multiple_of((1 - core) * half + q * width, width), width)
            stage[slot, :, q * width : (q + 1) * width] = dot(gu[rows, :], w[cols, :], (1, 1)).astype(stage.dtype)
        term_copy(b, step, i, slot).start()
        for q in range(2):
            cols = pl.ds(pl.multiple_of(core * half + q * width, width), width)
            own[:, q * width : (q + 1) * width] = dot(gu[rows, :], w[cols, :], (1, 1))
        term_copy(b, step, i, slot).wait_recv()

    def summed(step, i, p):
        r = pl.ds(row_at(step, i, p), PART)
        return own[pl.ds(pl.multiple_of(p * PART, PART), PART), :] + dx[r, mine].astype(jnp.float32)

    def far_copy(i, side):
        return remote(
            sendbuf.at[i, side], far.at[side, i], rs_send.at[i, side], far_recv.at[side, i], device_at(steps[side])
        )

    def near_copy(j, i, p, side, step):
        return remote(
            sendbuf.at[2 + j, p], near.at[side, i, p], rs_send.at[2 + j, p], near_recv.at[side, i, p], device_at(step)
        )

    in_wd.wait()

    @pl.loop(0, 2)
    def _(i):
        hidden_block(i, 2, i)
        start_rows(2 + i, 1 + 2 * i, 0)
        x_copy(i).start()

        @pl.when(i == 0)
        def _():
            in_wg.wait()
            in_wu.wait()
            pl.semaphore_wait(barrier, 3)

        term_block(i, 2, i, i)
        for p in range(2):
            sendbuf[i, p] = summed(2, i, p).astype(sendbuf.dtype)
            far_copy(i, p).start()

    @pl.loop(0, 4)
    def _(j):
        side, i = lax.rem(j, 2), lax.div(j, 2)
        step = 1 + 2 * side
        hidden_block(2 + j, step, i)

        @pl.when(j < 2)
        def _():
            start_rows(4 + j, step, 1)

        @pl.when(j >= 2)
        def _():
            start_rows(4 + j, 0, side)

        x_copy(2 + j).start()
        term_copy(0, step, i, side).wait_send()
        term_block(2 + j, step, i, side)
        plain = 1 - side
        sendbuf[2 + j, plain] = summed(step, i, plain).astype(sendbuf.dtype)
        near_copy(j, i, plain, side, step).start()
        remote(sendbuf.at[0, 0], far.at[side, i], rs_send.at[0, 0], far_recv.at[side, i], peer).wait_recv()
        sendbuf[2 + j, side] = (summed(step, i, side) + far[side, i].astype(jnp.float32)).astype(sendbuf.dtype)
        near_copy(j, i, side, side, step).start()

    for i in range(2):
        hidden_block(6 + i, 0, i)
        x_copy(6 + i).start()

    @pl.loop(0, 4)
    def _(t):
        cols = pl.ds(pl.multiple_of(t * (d // 4), d // 4), d // 4)
        dwd[:, cols] = dot(hid_t[...], dy[:, cols], (1, 0)).astype(dwd.dtype)

    def direct(i, p, side):
        r = pl.ds(row_at(0, i, p), PART)
        return remote(
            dx.at[r, mine], dx.at[r, mine], ag_send.at[side, i, p], ag_recv.at[side, i, p], device_at(steps[side])
        )

    def forward(i, side):
        r = pl.ds(row_at(steps[1 - side], i, side), PART)
        return remote(dx.at[r, mine], dx.at[r, mine], fwd_send.at[side, i], fwd_recv.at[side, i], device_at(steps[side]))

    peers = []

    def share(step, i, p, rows=PART):
        k, r = len(peers), pl.ds(row_at(step, i, p), rows)
        peers.append(remote(dx.at[r, mine], dx.at[r, mine], peer_send.at[k], peer_recv.at[k], peer))
        peers[-1].start()

    def own_block(i):
        term_copy(0, 0, i, i).wait_send()
        term_block(6 + i, 0, i, i)
        for p in range(2):
            for side in range(2):
                near_copy(0, i, p, side, 0).wait_recv()
            total = summed(0, i, p)
            for side in range(2):
                total += near[side, i, p].astype(jnp.float32)
            dx[pl.ds(row_at(0, i, p), PART), mine] = total.astype(dx.dtype)
            direct(i, p, p).start()
        direct(i, 1, 0).start()
        direct(i, 0, 1).start()
        share(0, i, 0, BLOCK)

    def weight_tiles(lo, hi):
        @pl.loop(lo, hi)
        def _(t):
            cols = pl.ds(pl.multiple_of(t * TILE, TILE), TILE)
            dw[cols, :] = dot(x[:, cols], gu[...], (0, 0)).astype(dw.dtype)

    def relay(i):
        for side in range(2):
            direct(i, side, side).wait_recv()
            forward(i, side).start()
            share(steps[1 - side], i, side)

    def keep(i):
        for side in range(2):
            direct(i, 1 - side, side).wait_recv()
            share(steps[1 - side], i, 1 - side)

    def last(i):
        for side in range(2):
            forward(i, side).wait_recv()
            share(2, i, side)

    own_block(0)
    for b in range(8):
        x_copy(b).wait()
    weight_tiles(0, 2)
    own_block(1)
    weight_tiles(2, 4)
    relay(0)
    weight_tiles(4, 5)
    keep(0)
    weight_tiles(5, 7)
    relay(1)
    weight_tiles(7, d // TILE)
    keep(1)
    last(0)
    last(1)

    for i in range(2):
        term_copy(0, 0, i, i).wait_send()
        for p in range(2):
            far_copy(i, p).wait_send()
            for side in range(2):
                near_copy(2 * i + side, i, p, side, steps[side]).wait_send()
                direct(i, p, side).wait_send()
        for side in range(2):
            forward(i, side).wait_send()
    for c in peers:
        c.wait()


def write_kernel(dx, dw, dwd, dx_hbm, dwg_hbm, dwu_hbm, dwd_hbm, sem):
    f = dwd.shape[0]
    copies = [
        pltpu.make_async_copy(dx, dx_hbm, sem.at[0]),
        pltpu.make_async_copy(dw.at[:, pl.ds(0, f)], dwg_hbm, sem.at[1]),
        pltpu.make_async_copy(dw.at[:, pl.ds(f, f)], dwu_hbm, sem.at[2]),
        pltpu.make_async_copy(dwd, dwd_hbm, sem.at[3]),
    ]
    for c in copies:
        c.start()
    for c in copies:
        c.wait()


def solution(mesh):
    assert mesh.shape["tp"] == 2 * CHIPS

    def step(x, dy, gate, up, w_gate, w_up, w_down):
        tokens, d = x.shape
        f = w_down.shape[0]
        assert tokens == CHIPS * 2 * BLOCK
        half = d // 2
        bf16, f32 = jnp.bfloat16, jnp.float32
        dma = pltpu.SemaphoreType.DMA
        vmem, hbm = pl.BlockSpec(memory_space=pltpu.VMEM), pl.BlockSpec(memory_space=pltpu.HBM)
        dx, dw, dwd = pl.pallas_call(
            main_kernel,
            name="block_grads",
            out_shape=(pltpu.VMEM((tokens, d), bf16), pltpu.VMEM((d, 2 * f), bf16), pltpu.VMEM((f, d), bf16)),
            in_specs=[hbm] * 7,
            out_specs=(vmem,) * 3,
            scratch_shapes=[
                pltpu.VMEM((tokens, d), bf16),
                pltpu.VMEM((tokens, d), bf16),
                pltpu.VMEM((tokens, 2 * f), bf16),
                pltpu.VMEM((d, 2 * f), bf16),
                pltpu.VMEM((f, d), bf16),
                pltpu.VMEM((BLOCK, f), bf16),
                pltpu.VMEM((f, tokens), bf16),
                pltpu.VMEM((BLOCK, f), f32),
                pltpu.VMEM((BLOCK, half), f32),
                pltpu.VMEM((2, BLOCK, half), bf16),
                pltpu.VMEM((6, 2, PART, half), bf16),
                pltpu.VMEM((2, 2, PART, half), bf16),
                pltpu.VMEM((2, 2, 2, PART, half), bf16),
                dma((3,)),
                dma((4, 8)),
                dma((2,)),
                dma((8,)),
                dma((6, 2)),
                dma((2, 2)),
                dma((2, 2, 2)),
                dma((2, 2, 2)),
                dma((2, 2, 2)),
                dma((2, 2)),
                dma((2, 2)),
                dma((14,)),
                dma((14,)),
            ],
            compiler_params=pltpu.CompilerParams(collective_id=0, has_side_effects=True, vmem_limit_bytes=44 * 2**20),
        )(x, dy, gate, up, w_gate, w_up, w_down)
        return pl.pallas_call(
            write_kernel,
            name="write_out",
            out_shape=tuple(
                jax.ShapeDtypeStruct(s, bf16) for s in ((tokens, d), (d, f), (d, f), (f, d))
            ),
            in_specs=[vmem] * 3,
            out_specs=(hbm,) * 4,
            scratch_shapes=[dma((4,))],
            compiler_params=pltpu.CompilerParams(vmem_limit_bytes=20 * 2**20),
        )(dx, dw, dwd)

    tokens, columns, rows = P("dp", None), P(None, "tp"), P("tp", None)
    return jax.shard_map(
        step,
        mesh=mesh,
        in_specs=(tokens, tokens, P("dp", "tp"), P("dp", "tp"), columns, columns, rows),
        out_specs=(tokens, P("dp", "tp"), P("dp", "tp"), P(("dp", "tp"), None)),
        check_vma=False,
    )
```

time: 162 us -> 94.7 us (0.58)
  Pallas kernels: 0 us -> 93.9 us
  matrix products: 74.1 us -> 0 us
  waiting for transfers between devices: 60.1 us -> 0 us
  local copies, waits for them, and re-layouts: 13.8 us -> 0 us
  between operations: 14.1 us -> 0.8 us
    pallas_call x0 -> x2, Pallas kernels: none -> 93.9 us  [the longest x1 88 us: step(): pl.pallas_call(main_kernel, name='block_grads', out_shape=(pltpu.VMEM((to...]
    dot_general x6 -> x0, matrix products: 74.1 us -> none  [the longest x1 16 us: step(): jnp.dot(d_up, w_up.T, preferred_element_type=jnp.float32)]
    psum x1 -> x0, waiting for transfers between devices: 60 us -> none  [step(): dx = lax.psum(term.astype(jnp.bfloat16), 'tp')]
    unnamed x11 -> x0, local copies, waits for them, and re-layouts: 13.8 us -> none
  transfers between devices with their start and end apart: 1 -> 0, of which waited for: 1 -> 0; matrix products, arithmetic and copies ran while one was open for 24% -> 0% of each run, Pallas kernels for 0% -> 0%
where the time goes in v1:
time: 94.7 us
  Pallas kernels  93.9 us (99%)
    pallas_call x1, Pallas kernels, step(): pl.pallas_call(main_kernel, name='block_grads', out_shape=(pltpu.VMEM((to...  88 us
    pallas_call x1, Pallas kernels, step(): pl.pallas_call(write_kernel, name='write_out', out_shape=tuple((jax.Shape...  5.87 us

profile of v1, /device:TPU:113, one launch (start us, length us, event | category | flops | bytes accessed | tf_op | source)
XLA Modules:
  0.0 94.7 jit_solution(5252223336468766097)
XLA Ops:
  0.6 88.0 %block_grads.1 = (bf16[2048,2048]{1,0:T(8,128)(2,1)S(1)}, bf16[2048,1280]{1,0:T(8,128)(2,1)S(1)}, bf16[640,2048]{1,0:T(8,128)(2,1)S(1)}) custom-call(bf16[2048,2048]{1,0:T(8,128)(2,1)} %x_hbm.1, bf16[2048,2048]{1,0:T(8,128)(2,1)} %dy_hbm.1, bf16[2048,640]{1,0:T(8,128)(2,1)} %gate_hbm.1, bf16[2048,640]{1,0:T(8,128)(2,1)} %up_hbm.1, bf16[2048,640]{1,0:T(8,128)(2,1)} %wg_hbm.1, ...), custom_call_target="tpu_custom_call" | custom-call | tf_op jit(solution)/shard_map/block_grads/pallas_call | solution.py:296
  88.6 5.9 %write_out.1 = (bf16[2048,2048]{1,0:T(8,128)(2,1)}, bf16[2048,640]{1,0:T(8,128)(2,1)}, bf16[2048,640]{1,0:T(8,128)(2,1)}, bf16[640,2048]{1,0:T(8,128)(2,1)}) custom-call(bf16[2048,2048]{1,0:T(8,128)(2,1)S(1)} %get-tuple-element.7.dx, bf16[2048,1280]{1,0:T(8,128)(2,1)S(1)} %get-tuple-element.8.dw, bf16[640,2048]{1,0:T(8,128)(2,1)S(1)} %get-tuple-element.9.dwd), custom_call_target="tpu_custom_call" | custom-call | tf_op jit(solution)/shard_map/write_out/pallas_call | solution.py:332

commit v2 on v1

--- a/solution.py
+++ b/solution.py
@@ -11,6 +11,8 @@
 CHIPS = 4
 BLOCK = 256
 PART = BLOCK // 2
+PIECES = 2
+SHARE = 32
 STRIP = 32
 TILE = 256
 
@@ -34,11 +36,11 @@
     f = wd.shape[0]
     half = d // 2
     chunk_rows = tokens // CHIPS
+    width = half // PIECES
     me = lax.axis_index("tp")
     chip, core = lax.div(me, 2), lax.rem(me, 2)
     peer = chip * 2 + 1 - core
     mine = pl.ds(pl.multiple_of(core * half, half), half)
-    theirs = pl.ds(pl.multiple_of((1 - core) * half, half), half)
 
     def chip_at(step):
         return lax.rem(chip + step, CHIPS)
@@ -103,60 +105,84 @@
 
         hid_t[:, pl.ds(pl.multiple_of(start, BLOCK), BLOCK)] = hid[...].T
 
-    def term_copy(b, step, i, slot):
+    def cols_of(c, q):
+        return pl.ds(pl.multiple_of(c * half + q * width, width), width)
+
+    def term_copy(b, step, i, slot, q):
         rows = pl.ds(row_at(step, i), BLOCK)
-        return remote(stage.at[slot], dx.at[rows, theirs], term_send.at[slot], term_recv.at[b], peer)
-
-    def term_block(b, step, i, slot):
+        return remote(
+            stage.at[slot, q], dx.at[rows, cols_of(1 - core, q)], term_send.at[slot, q], term_recv.at[b, q], peer
+        )
+
+    def term_other(b, step, i, slot):
         rows = pl.ds(row_at(step, i), BLOCK)
-        width = half // 2
-        for q in range(2):
-            cols = pl.ds(pl.multiple_of((1 - core) * half + q * width, width), width)
-            stage[slot, :, q * width : (q + 1) * width] = dot(gu[rows, :], w[cols, :], (1, 1)).astype(stage.dtype)
-        term_copy(b, step, i, slot).start()
-        for q in range(2):
-            cols = pl.ds(pl.multiple_of(core * half + q * width, width), width)
-            own[:, q * width : (q + 1) * width] = dot(gu[rows, :], w[cols, :], (1, 1))
-        term_copy(b, step, i, slot).wait_recv()
-
-    def summed(step, i, p):
+        for q in range(PIECES):
+            stage[slot, q] = dot(gu[rows, :], w[cols_of(1 - core, q), :], (1, 1)).astype(stage.dtype)
+            term_copy(b, step, i, slot, q).start()
+
+    def term_own(step, i, slot):
+        rows = pl.ds(row_at(step, i), BLOCK)
+        for q in range(PIECES):
+            own[slot, q] = dot(gu[rows, :], w[cols_of(core, q), :], (1, 1))
+
+    def stage_free(slot):
+        for q in range(PIECES):
+            term_copy(0, 0, 0, slot, q).wait_send()
+
+    def summed(step, i, p, q, slot):
         r = pl.ds(row_at(step, i, p), PART)
-        return own[pl.ds(pl.multiple_of(p * PART, PART), PART), :] + dx[r, mine].astype(jnp.float32)
-
-    def far_copy(i, side):
-        return remote(
-            sendbuf.at[i, side], far.at[side, i], rs_send.at[i, side], far_recv.at[side, i], device_at(steps[side])
-        )
-
-    def near_copy(j, i, p, side, step):
-        return remote(
-            sendbuf.at[2 + j, p], near.at[side, i, p], rs_send.at[2 + j, p], near_recv.at[side, i, p], device_at(step)
-        )
+        mine_here = own[slot, q, pl.ds(pl.multiple_of(p * PART, PART), PART), :]
+        return mine_here + dx[r, cols_of(core, q)].astype(jnp.float32)
+
+    def far_copy(i, side, q):
+        return remote(
+            sendbuf.at[i, side, q],
+            far.at[side, i, q],
+            rs_send.at[i, side, q],
+            far_recv.at[side, i, q],
+            device_at(steps[side]),
+        )
+
+    def near_copy(j, i, p, q, side, step):
+        return remote(
+            sendbuf.at[2 + j, p, q],
+            near.at[side, i, p, q],
+            rs_send.at[2 + j, p, q],
+            near_recv.at[side, i, p, q],
+            device_at(step),
+        )
+
+    def finish_far(i):
+        for q in range(PIECES):
+            term_copy(i, 2, i, i, q).wait_recv()
+            for p in range(2):
+                sendbuf[i, p, q] = summed(2, i, p, q, i).astype(sendbuf.dtype)
+                far_copy(i, p, q).start()
 
     in_wd.wait()
 
-    @pl.loop(0, 2)
-    def _(i):
-        hidden_block(i, 2, i)
-        start_rows(2 + i, 1 + 2 * i, 0)
-        x_copy(i).start()
-
-        @pl.when(i == 0)
-        def _():
-            in_wg.wait()
-            in_wu.wait()
-            pl.semaphore_wait(barrier, 3)
-
-        term_block(i, 2, i, i)
-        for p in range(2):
-            sendbuf[i, p] = summed(2, i, p).astype(sendbuf.dtype)
-            far_copy(i, p).start()
+    hidden_block(0, 2, 0)
+    start_rows(2, 1, 0)
+    x_copy(0).start()
+    in_wg.wait()
+    in_wu.wait()
+    pl.semaphore_wait(barrier, 3)
+    term_other(0, 2, 0, 0)
+    term_own(2, 0, 0)
+    finish_far(0)
+
+    hidden_block(1, 2, 1)
+    start_rows(3, 3, 0)
+    x_copy(1).start()
+    term_other(1, 2, 1, 1)
+    hidden_block(2, 1, 0)
+    term_own(2, 1, 1)
+    finish_far(1)
 
     @pl.loop(0, 4)
     def _(j):
         side, i = lax.rem(j, 2), lax.div(j, 2)
         step = 1 + 2 * side
-        hidden_block(2 + j, step, i)
 
         @pl.when(j < 2)
         def _():
@@ -167,18 +193,32 @@
             start_rows(4 + j, 0, side)
 
         x_copy(2 + j).start()
-        term_copy(0, step, i, side).wait_send()
-        term_block(2 + j, step, i, side)
+        stage_free(side)
+        term_other(2 + j, step, i, side)
+        more = 1 - lax.div(j, 3)
+        hidden_block(3 + j, (3 - 2 * side) * more, lax.div(j + 1, 2) * more)
+        term_own(step, i, side)
         plain = 1 - side
-        sendbuf[2 + j, plain] = summed(step, i, plain).astype(sendbuf.dtype)
-        near_copy(j, i, plain, side, step).start()
-        remote(sendbuf.at[0, 0], far.at[side, i], rs_send.at[0, 0], far_recv.at[side, i], peer).wait_recv()
-        sendbuf[2 + j, side] = (summed(step, i, side) + far[side, i].astype(jnp.float32)).astype(sendbuf.dtype)
-        near_copy(j, i, side, side, step).start()
-
-    for i in range(2):
-        hidden_block(6 + i, 0, i)
-        x_copy(6 + i).start()
+        for q in range(PIECES):
+            term_copy(2 + j, step, i, side, q).wait_recv()
+            sendbuf[2 + j, plain, q] = summed(step, i, plain, q, side).astype(sendbuf.dtype)
+            near_copy(j, i, plain, q, side, step).start()
+        for q in range(PIECES):
+            remote(sendbuf.at[0, 0, 0], far.at[side, i, q], rs_send.at[0, 0, 0], far_recv.at[side, i, q], peer).wait_recv()
+            sendbuf[2 + j, side, q] = (
+                summed(step, i, side, q, side) + far[side, i, q].astype(jnp.float32)
+            ).astype(sendbuf.dtype)
+            near_copy(j, i, side, q, side, step).start()
+
+    x_copy(6).start()
+    x_copy(7).start()
+    stage_free(0)
+    term_other(6, 0, 0, 0)
+    hidden_block(7, 0, 1)
+    term_own(0, 0, 0)
+    stage_free(1)
+    term_other(7, 0, 1, 1)
+    term_own(0, 1, 1)
 
     @pl.loop(0, 4)
     def _(t):
@@ -191,27 +231,29 @@
             dx.at[r, mine], dx.at[r, mine], ag_send.at[side, i, p], ag_recv.at[side, i, p], device_at(steps[side])
         )
 
-    def forward(i, side):
-        r = pl.ds(row_at(steps[1 - side], i, side), PART)
-        return remote(dx.at[r, mine], dx.at[r, mine], fwd_send.at[side, i], fwd_recv.at[side, i], device_at(steps[side]))
+    def forward(i, side, k):
+        r = pl.ds(pl.multiple_of(row_at(steps[1 - side], i, side) + k * SHARE, SHARE), SHARE)
+        return remote(
+            dx.at[r, mine], dx.at[r, mine], fwd_send.at[side, i, k], fwd_recv.at[side, i, k], device_at(steps[side])
+        )
 
     peers = []
 
-    def share(step, i, p, rows=PART):
-        k, r = len(peers), pl.ds(row_at(step, i, p), rows)
-        peers.append(remote(dx.at[r, mine], dx.at[r, mine], peer_send.at[k], peer_recv.at[k], peer))
+    def share(step, i, p, rows=PART, k=0):
+        n, r = len(peers), pl.ds(pl.multiple_of(row_at(step, i, p) + k * SHARE, SHARE), rows)
+        peers.append(remote(dx.at[r, mine], dx.at[r, mine], peer_send.at[n], peer_recv.at[n], peer))
         peers[-1].start()
 
     def own_block(i):
-        term_copy(0, 0, i, i).wait_send()
-        term_block(6 + i, 0, i, i)
+        for q in range(PIECES):
+            term_copy(6 + i, 0, i, i, q).wait_recv()
         for p in range(2):
-            for side in range(2):
-                near_copy(0, i, p, side, 0).wait_recv()
-            total = summed(0, i, p)
-            for side in range(2):
-                total += near[side, i, p].astype(jnp.float32)
-            dx[pl.ds(row_at(0, i, p), PART), mine] = total.astype(dx.dtype)
+            for q in range(PIECES):
+                total = summed(0, i, p, q, i)
+                for side in range(2):
+                    near_copy(0, i, p, q, side, 0).wait_recv()
+                    total += near[side, i, p, q].astype(jnp.float32)
+                dx[pl.ds(row_at(0, i, p), PART), cols_of(core, q)] = total.astype(dx.dtype)
             direct(i, p, p).start()
         direct(i, 1, 0).start()
         direct(i, 0, 1).start()
@@ -226,7 +268,8 @@
     def relay(i):
         for side in range(2):
             direct(i, side, side).wait_recv()
-            forward(i, side).start()
+            for k in range(PART // SHARE):
+                forward(i, side, k).start()
             share(steps[1 - side], i, side)
 
     def keep(i):
@@ -235,35 +278,36 @@
             share(steps[1 - side], i, 1 - side)
 
     def last(i):
-        for side in range(2):
-            forward(i, side).wait_recv()
-            share(2, i, side)
+        for k in range(PART // SHARE):
+            for side in range(2):
+                forward(i, side, k).wait_recv()
+                share(2, i, side, SHARE, k)
 
     own_block(0)
     for b in range(8):
         x_copy(b).wait()
-    weight_tiles(0, 2)
+    weight_tiles(0, 5)
     own_block(1)
-    weight_tiles(2, 4)
+    weight_tiles(5, d // TILE)
     relay(0)
-    weight_tiles(4, 5)
     keep(0)
-    weight_tiles(5, 7)
     relay(1)
-    weight_tiles(7, d // TILE)
     keep(1)
     last(0)
     last(1)
 
     for i in range(2):
-        term_copy(0, 0, i, i).wait_send()
+        stage_free(i)
         for p in range(2):
-            far_copy(i, p).wait_send()
+            for q in range(PIECES):
+                far_copy(i, p, q).wait_send()
+                for side in range(2):
+                    near_copy(2 * i + side, i, p, q, side, steps[side]).wait_send()
             for side in range(2):
-                near_copy(2 * i + side, i, p, side, steps[side]).wait_send()
                 direct(i, p, side).wait_send()
         for side in range(2):
-            forward(i, side).wait_send()
+            for k in range(PART // SHARE):
+                forward(i, side, k).wait_send()
     for c in peers:
         c.wait()
 
@@ -308,26 +352,26 @@
                 pltpu.VMEM((BLOCK, f), bf16),
                 pltpu.VMEM((f, tokens), bf16),
                 pltpu.VMEM((BLOCK, f), f32),
-                pltpu.VMEM((BLOCK, half), f32),
-                pltpu.VMEM((2, BLOCK, half), bf16),
-                pltpu.VMEM((6, 2, PART, half), bf16),
-                pltpu.VMEM((2, 2, PART, half), bf16),
-                pltpu.VMEM((2, 2, 2, PART, half), bf16),
+                pltpu.VMEM((2, PIECES, BLOCK, half // PIECES), f32),
+                pltpu.VMEM((2, PIECES, BLOCK, half // PIECES), bf16),
+                pltpu.VMEM((6, 2, PIECES, PART, half // PIECES), bf16),
+                pltpu.VMEM((2, 2, PIECES, PART, half // PIECES), bf16),
+                pltpu.VMEM((2, 2, 2, PIECES, PART, half // PIECES), bf16),
                 dma((3,)),
                 dma((4, 8)),
-                dma((2,)),
-                dma((8,)),
-                dma((6, 2)),
-                dma((2, 2)),
+                dma((2, PIECES)),
+                dma((8, PIECES)),
+                dma((6, 2, PIECES)),
+                dma((2, 2, PIECES)),
+                dma((2, 2, 2, PIECES)),
                 dma((2, 2, 2)),
                 dma((2, 2, 2)),
-                dma((2, 2, 2)),
-                dma((2, 2)),
-                dma((2, 2)),
-                dma((14,)),
-                dma((14,)),
+                dma((2, 2, PART // SHARE)),
+                dma((2, 2, PART // SHARE)),
+                dma((10 + 4 * PART // SHARE,)),
+                dma((10 + 4 * PART // SHARE,)),
             ],
-            compiler_params=pltpu.CompilerParams(collective_id=0, has_side_effects=True, vmem_limit_bytes=44 * 2**20),
+            compiler_params=pltpu.CompilerParams(collective_id=0, has_side_effects=True, vmem_limit_bytes=47 * 2**20),
         )(x, dy, gate, up, w_gate, w_up, w_down)
         return pl.pallas_call(
             write_kernel,

time: 94.7 us -> 93 us (0.982)
  Pallas kernels: 93.9 us -> 92.1 us
    pallas_call x1, Pallas kernels: 88 us -> 86.3 us  [step(): pl.pallas_call(main_kernel, name='block_grads', out_shape=(pltpu.VMEM((to...]
where the time goes in v2:
time: 93 us; the launch traced here: 92.9 us
  Pallas kernels  92.1 us (99%)
    pallas_call x1, Pallas kernels, step(): pl.pallas_call(main_kernel, name='block_grads', out_shape=(pltpu.VMEM((to...  86.3 us
    pallas_call x1, Pallas kernels, step(): pl.pallas_call(write_kernel, name='write_out', out_shape=tuple((jax.Shape...  5.87 us

profile of v2, /device:TPU:113, one launch (start us, length us, event | category | flops | bytes accessed | tf_op | source)
XLA Modules:
  0.0 92.9 jit_solution(12954938212524515213)
XLA Ops:
  0.6 86.3 %block_grads.1 = (bf16[2048,2048]{1,0:T(8,128)(2,1)S(1)}, bf16[2048,1280]{1,0:T(8,128)(2,1)S(1)}, bf16[640,2048]{1,0:T(8,128)(2,1)S(1)}) custom-call(bf16[2048,2048]{1,0:T(8,128)(2,1)} %x_hbm.1, bf16[2048,2048]{1,0:T(8,128)(2,1)} %dy_hbm.1, bf16[2048,640]{1,0:T(8,128)(2,1)} %gate_hbm.1, bf16[2048,640]{1,0:T(8,128)(2,1)} %up_hbm.1, bf16[2048,640]{1,0:T(8,128)(2,1)} %wg_hbm.1, ...), custom_call_target="tpu_custom_call" | custom-call | tf_op jit(solution)/shard_map/block_grads/pallas_call | solution.py:340
  86.9 5.9 %write_out.1 = (bf16[2048,2048]{1,0:T(8,128)(2,1)}, bf16[2048,640]{1,0:T(8,128)(2,1)}, bf16[2048,640]{1,0:T(8,128)(2,1)}, bf16[640,2048]{1,0:T(8,128)(2,1)}) custom-call(bf16[2048,2048]{1,0:T(8,128)(2,1)S(1)} %get-tuple-element.7.dx, bf16[2048,1280]{1,0:T(8,128)(2,1)S(1)} %get-tuple-element.8.dw, bf16[640,2048]{1,0:T(8,128)(2,1)S(1)} %get-tuple-element.9.dwd), custom_call_target="tpu_custom_call" | custom-call | tf_op jit(solution)/shard_map/write_out/pallas_call | solution.py:376

commit v3 on v2

--- a/solution.py
+++ b/solution.py
@@ -179,36 +179,39 @@
     term_own(2, 1, 1)
     finish_far(1)
 
-    @pl.loop(0, 4)
-    def _(j):
-        side, i = lax.rem(j, 2), lax.div(j, 2)
-        step = 1 + 2 * side
-
-        @pl.when(j < 2)
-        def _():
-            start_rows(4 + j, step, 1)
-
-        @pl.when(j >= 2)
-        def _():
-            start_rows(4 + j, 0, side)
-
-        x_copy(2 + j).start()
-        stage_free(side)
-        term_other(2 + j, step, i, side)
-        more = 1 - lax.div(j, 3)
-        hidden_block(3 + j, (3 - 2 * side) * more, lax.div(j + 1, 2) * more)
-        term_own(step, i, side)
-        plain = 1 - side
-        for q in range(PIECES):
-            term_copy(2 + j, step, i, side, q).wait_recv()
-            sendbuf[2 + j, plain, q] = summed(step, i, plain, q, side).astype(sendbuf.dtype)
-            near_copy(j, i, plain, q, side, step).start()
-        for q in range(PIECES):
-            remote(sendbuf.at[0, 0, 0], far.at[side, i, q], rs_send.at[0, 0, 0], far_recv.at[side, i, q], peer).wait_recv()
-            sendbuf[2 + j, side, q] = (
-                summed(step, i, side, q, side) + far[side, i, q].astype(jnp.float32)
-            ).astype(sendbuf.dtype)
-            near_copy(j, i, side, q, side, step).start()
+    @pl.loop(0, 2)
+    def _(i):
+        for side in range(2):
+            b, step, plain = 2 + 2 * i + side, steps[side], 1 - side
+
+            @pl.when(i == 0)
+            def _():
+                start_rows(4 + side, step, 1)
+
+            @pl.when(i == 1)
+            def _():
+                start_rows(6 + side, 0, side)
+
+            x_copy(b).start()
+            stage_free(side)
+            term_other(b, step, i, side)
+            if side == 0:
+                hidden_block(b + 1, steps[1], i)
+            else:
+                hidden_block(b + 1, 1 - i, 1 - i)
+            term_own(step, i, side)
+            for q in range(PIECES):
+                term_copy(b, step, i, side, q).wait_recv()
+                sendbuf[b, plain, q] = summed(step, i, plain, q, side).astype(sendbuf.dtype)
+                near_copy(b - 2, i, plain, q, side, step).start()
+        for q in range(PIECES):
+            for side in range(2):
+                b, step = 2 + 2 * i + side, steps[side]
+                far_copy(i, side, q).wait_recv()
+                sendbuf[b, side, q] = (
+                    summed(step, i, side, q, side) + far[side, i, q].astype(jnp.float32)
+                ).astype(sendbuf.dtype)
+                near_copy(b - 2, i, side, q, side, step).start()
 
     x_copy(6).start()
     x_copy(7).start()

time: 93 us -> 93.1 us (level)
  no operation moved by 1% of the time
where the time goes in v3:
time: 93.1 us; the launch traced here: 93 us
  Pallas kernels  92.2 us (99%)
    pallas_call x1, Pallas kernels, step(): pl.pallas_call(main_kernel, name='block_grads', out_shape=(pltpu.VMEM((to...  86.4 us
    pallas_call x1, Pallas kernels, step(): pl.pallas_call(write_kernel, name='write_out', out_shape=tuple((jax.Shape...  5.87 us

profile of v3, /device:TPU:113, one launch (start us, length us, event | category | flops | bytes accessed | tf_op | source)
XLA Modules:
  0.0 93.0 jit_solution(17570179014083893375)
XLA Ops:
  0.6 86.4 %block_grads.1 = (bf16[2048,2048]{1,0:T(8,128)(2,1)S(1)}, bf16[2048,1280]{1,0:T(8,128)(2,1)S(1)}, bf16[640,2048]{1,0:T(8,128)(2,1)S(1)}) custom-call(bf16[2048,2048]{1,0:T(8,128)(2,1)} %x_hbm.1, bf16[2048,2048]{1,0:T(8,128)(2,1)} %dy_hbm.1, bf16[2048,640]{1,0:T(8,128)(2,1)} %gate_hbm.1, bf16[2048,640]{1,0:T(8,128)(2,1)} %up_hbm.1, bf16[2048,640]{1,0:T(8,128)(2,1)} %wg_hbm.1, ...), custom_call_target="tpu_custom_call" | custom-call | tf_op jit(solution)/shard_map/block_grads/pallas_call | solution.py:343
  87.0 5.9 %write_out.1 = (bf16[2048,2048]{1,0:T(8,128)(2,1)}, bf16[2048,640]{1,0:T(8,128)(2,1)}, bf16[2048,640]{1,0:T(8,128)(2,1)}, bf16[640,2048]{1,0:T(8,128)(2,1)}) custom-call(bf16[2048,2048]{1,0:T(8,128)(2,1)S(1)} %get-tuple-element.7.dx, bf16[2048,1280]{1,0:T(8,128)(2,1)S(1)} %get-tuple-element.8.dw, bf16[640,2048]{1,0:T(8,128)(2,1)S(1)} %get-tuple-element.9.dwd), custom_call_target="tpu_custom_call" | custom-call | tf_op jit(solution)/shard_map/write_out/pallas_call | solution.py:379

commit v4 on v3

--- a/solution.py
+++ b/solution.py
@@ -29,7 +29,7 @@
     x_hbm, dy_hbm, gate_hbm, up_hbm, wg_hbm, wu_hbm, wd_hbm,
     dx, dw, dwd,
     x, dy, gu, w, wd, hid, hid_t, dh, own, stage, sendbuf, far, near,
-    in_sem, row_sem, term_send, term_recv, rs_send, far_recv, near_recv,
+    in_sem, row_sem, x_sem, term_send, term_recv, rs_send, far_recv, near_recv,
     ag_send, ag_recv, fwd_send, fwd_recv, peer_send, peer_recv,
 ):
     tokens, d = x.shape
@@ -62,77 +62,94 @@
     def row_at(step, i, p=0):
         return pl.multiple_of(chip_at(step) * chunk_rows + i * BLOCK + p * PART, PART)
 
-    def row_copies(b, step, i):
-        r = pl.ds(row_at(step, i), BLOCK)
-        return (
-            pltpu.make_async_copy(dy_hbm.at[r], dy.at[r], row_sem.at[0, b]),
-            pltpu.make_async_copy(gate_hbm.at[r], gu.at[r, pl.ds(0, f)], row_sem.at[1, b]),
-            pltpu.make_async_copy(up_hbm.at[r], gu.at[r, pl.ds(f, f)], row_sem.at[2, b]),
-        )
-
-    def start_rows(b, step, i):
-        for c in row_copies(b, step, i):
+    def far_rows(i):
+        return row_at(2, i, 0), row_at(2, i, 1)
+
+    def near_rows(i, k):
+        return row_at(1, i, 1 - k), row_at(CHIPS - 1, i, k)
+
+    def own_rows(i):
+        return row_at(0, i, 0), row_at(0, i, 1)
+
+    def row_copies(b, rows):
+        copies = []
+        for p in range(2):
+            r = pl.ds(rows[p], PART)
+            copies += [
+                pltpu.make_async_copy(dy_hbm.at[r], dy.at[r], row_sem.at[0, b, p]),
+                pltpu.make_async_copy(gate_hbm.at[r], gu.at[r, pl.ds(0, f)], row_sem.at[1, b, p]),
+                pltpu.make_async_copy(up_hbm.at[r], gu.at[r, pl.ds(f, f)], row_sem.at[2, b, p]),
+            ]
+        return copies
+
+    def start_rows(b, rows):
+        for c in row_copies(b, rows):
             c.start()
 
     def x_copy(b):
         r = pl.ds(pl.multiple_of(b * BLOCK, BLOCK), BLOCK)
-        return pltpu.make_async_copy(x_hbm.at[r], x.at[r], row_sem.at[3, b])
+        return pltpu.make_async_copy(x_hbm.at[r], x.at[r], x_sem.at[b])
 
     in_wd = pltpu.make_async_copy(wd_hbm, wd, in_sem.at[0])
     in_wg = pltpu.make_async_copy(wg_hbm, w.at[:, pl.ds(0, f)], in_sem.at[1])
     in_wu = pltpu.make_async_copy(wu_hbm, w.at[:, pl.ds(f, f)], in_sem.at[2])
     in_wd.start()
-    start_rows(0, 2, 0)
+    start_rows(0, far_rows(0))
     in_wg.start()
     in_wu.start()
-    start_rows(1, 2, 1)
-
-    def hidden_block(b, step, i):
-        start = row_at(step, i)
-        for c in row_copies(b, step, i):
+    start_rows(1, far_rows(1))
+
+    def both(ref, rows):
+        return jnp.concatenate([ref[pl.ds(r, PART), :] for r in rows], axis=0)
+
+    def hidden_block(b, rows):
+        for c in row_copies(b, rows):
             c.wait()
-        dh[...] = dot(dy[pl.ds(start, BLOCK), :], wd[...], (1, 1))
-
-        @pl.loop(0, BLOCK // STRIP)
-        def _(s):
-            here = pl.ds(pl.multiple_of(s * STRIP, STRIP), STRIP)
-            r = pl.ds(pl.multiple_of(start + s * STRIP, STRIP), STRIP)
-            h, back = jax.vjp(act, gu[r, pl.ds(0, f)].astype(jnp.float32), gu[r, pl.ds(f, f)].astype(jnp.float32))
-            d_gate, d_up = back(dh[here, :])
-            gu[r, pl.ds(0, f)] = d_gate.astype(gu.dtype)
-            gu[r, pl.ds(f, f)] = d_up.astype(gu.dtype)
-            hid[here, :] = h.astype(hid.dtype)
-
-        hid_t[:, pl.ds(pl.multiple_of(start, BLOCK), BLOCK)] = hid[...].T
+        dh[...] = dot(both(dy, rows), wd[...], (1, 1))
+        for p in range(2):
+
+            @pl.loop(0, PART // STRIP)
+            def _(s):
+                here = pl.ds(pl.multiple_of(p * PART + s * STRIP, STRIP), STRIP)
+                r = pl.ds(pl.multiple_of(rows[p] + s * STRIP, STRIP), STRIP)
+                h, back = jax.vjp(act, gu[r, pl.ds(0, f)].astype(jnp.float32), gu[r, pl.ds(f, f)].astype(jnp.float32))
+                d_gate, d_up = back(dh[here, :])
+                gu[r, pl.ds(0, f)] = d_gate.astype(gu.dtype)
+                gu[r, pl.ds(f, f)] = d_up.astype(gu.dtype)
+                hid[here, :] = h.astype(hid.dtype)
+
+            hid_t[:, pl.ds(rows[p], PART)] = hid[p * PART : (p + 1) * PART, :].T
 
     def cols_of(c, q):
         return pl.ds(pl.multiple_of(c * half + q * width, width), width)
 
-    def term_copy(b, step, i, slot, q):
-        rows = pl.ds(row_at(step, i), BLOCK)
+    def term_copy(b, rows, slot, q, p):
         return remote(
-            stage.at[slot, q], dx.at[rows, cols_of(1 - core, q)], term_send.at[slot, q], term_recv.at[b, q], peer
-        )
-
-    def term_other(b, step, i, slot):
-        rows = pl.ds(row_at(step, i), BLOCK)
+            stage.at[slot, q, pl.ds(p * PART, PART)],
+            dx.at[pl.ds(rows[p], PART), cols_of(1 - core, q)],
+            term_send.at[slot, q, p],
+            term_recv.at[b, q, p],
+            peer,
+        )
+
+    def term_other(b, rows, slot):
         for q in range(PIECES):
-            stage[slot, q] = dot(gu[rows, :], w[cols_of(1 - core, q), :], (1, 1)).astype(stage.dtype)
-            term_copy(b, step, i, slot, q).start()
-
-    def term_own(step, i, slot):
-        rows = pl.ds(row_at(step, i), BLOCK)
+            stage[slot, q] = dot(both(gu, rows), w[cols_of(1 - core, q), :], (1, 1)).astype(stage.dtype)
+            for p in range(2):
+                term_copy(b, rows, slot, q, p).start()
+
+    def term_own(rows, slot):
         for q in range(PIECES):
-            own[slot, q] = dot(gu[rows, :], w[cols_of(core, q), :], (1, 1))
+            own[slot, q] = dot(both(gu, rows), w[cols_of(core, q), :], (1, 1))
 
     def stage_free(slot):
         for q in range(PIECES):
-            term_copy(0, 0, 0, slot, q).wait_send()
-
-    def summed(step, i, p, q, slot):
-        r = pl.ds(row_at(step, i, p), PART)
-        mine_here = own[slot, q, pl.ds(pl.multiple_of(p * PART, PART), PART), :]
-        return mine_here + dx[r, cols_of(core, q)].astype(jnp.float32)
+            for p in range(2):
+                term_copy(0, far_rows(0), slot, q, p).wait_send()
+
+    def summed(b, rows, slot, q, p):
+        term_copy(b, rows, slot, q, p).wait_recv()
+        return own[slot, q, p * PART : (p + 1) * PART, :] + dx[pl.ds(rows[p], PART), cols_of(core, q)].astype(jnp.float32)
 
     def far_copy(i, side, q):
         return remote(
@@ -143,85 +160,75 @@
             device_at(steps[side]),
         )
 
-    def near_copy(j, i, p, q, side, step):
+    def near_copy(i, k, side, q):
+        b = 2 + 2 * i + k
         return remote(
-            sendbuf.at[2 + j, p, q],
-            near.at[side, i, p, q],
-            rs_send.at[2 + j, p, q],
-            near_recv.at[side, i, p, q],
-            device_at(step),
+            sendbuf.at[b, side, q],
+            near.at[side, i, k, q],
+            rs_send.at[b, side, q],
+            near_recv.at[side, i, k, q],
+            device_at(steps[side]),
         )
 
     def finish_far(i):
         for q in range(PIECES):
-            term_copy(i, 2, i, i, q).wait_recv()
-            for p in range(2):
-                sendbuf[i, p, q] = summed(2, i, p, q, i).astype(sendbuf.dtype)
-                far_copy(i, p, q).start()
+            for side in range(2):
+                sendbuf[i, side, q] = summed(i, far_rows(i), i, q, side).astype(sendbuf.dtype)
+                far_copy(i, side, q).start()
 
     in_wd.wait()
 
-    hidden_block(0, 2, 0)
-    start_rows(2, 1, 0)
+    hidden_block(0, far_rows(0))
+    start_rows(2, near_rows(0, 0))
     x_copy(0).start()
     in_wg.wait()
     in_wu.wait()
     pl.semaphore_wait(barrier, 3)
-    term_other(0, 2, 0, 0)
-    term_own(2, 0, 0)
+    term_other(0, far_rows(0), 0)
+    term_own(far_rows(0), 0)
     finish_far(0)
 
-    hidden_block(1, 2, 1)
-    start_rows(3, 3, 0)
+    hidden_block(1, far_rows(1))
+    start_rows(3, near_rows(0, 1))
     x_copy(1).start()
-    term_other(1, 2, 1, 1)
-    hidden_block(2, 1, 0)
-    term_own(2, 1, 1)
+    term_other(1, far_rows(1), 1)
+    hidden_block(2, near_rows(0, 0))
+    term_own(far_rows(1), 1)
     finish_far(1)
 
     @pl.loop(0, 2)
     def _(i):
-        for side in range(2):
-            b, step, plain = 2 + 2 * i + side, steps[side], 1 - side
-
-            @pl.when(i == 0)
-            def _():
-                start_rows(4 + side, step, 1)
-
-            @pl.when(i == 1)
-            def _():
-                start_rows(6 + side, 0, side)
-
+        m = 1 - i
+        coming = (
+            (row_at(m, m, m), row_at(3 * m, m, 1 - m)),
+            (row_at(m, 1, 0), row_at(3 * m, 1, 1)),
+        )
+        for k in range(2):
+            b, rows = 2 + 2 * i + k, near_rows(i, k)
+            start_rows(b + 2, coming[k])
             x_copy(b).start()
-            stage_free(side)
-            term_other(b, step, i, side)
-            if side == 0:
-                hidden_block(b + 1, steps[1], i)
-            else:
-                hidden_block(b + 1, 1 - i, 1 - i)
-            term_own(step, i, side)
+            stage_free(k)
+            term_other(b, rows, k)
+            hidden_block(b + 1, near_rows(i, 1) if k == 0 else coming[0])
+            term_own(rows, k)
             for q in range(PIECES):
-                term_copy(b, step, i, side, q).wait_recv()
-                sendbuf[b, plain, q] = summed(step, i, plain, q, side).astype(sendbuf.dtype)
-                near_copy(b - 2, i, plain, q, side, step).start()
-        for q in range(PIECES):
-            for side in range(2):
-                b, step = 2 + 2 * i + side, steps[side]
-                far_copy(i, side, q).wait_recv()
-                sendbuf[b, side, q] = (
-                    summed(step, i, side, q, side) + far[side, i, q].astype(jnp.float32)
-                ).astype(sendbuf.dtype)
-                near_copy(b - 2, i, side, q, side, step).start()
+                for side in range(2):
+                    total = summed(b, rows, k, q, side)
+                    if k == 1:
+                        far_copy(i, side, q).wait_recv()
+                        total += far[side, i, q].astype(jnp.float32)
+                    sendbuf[b, side, q] = total.astype(sendbuf.dtype)
+                    near_copy(i, k, side, q).start()
 
     x_copy(6).start()
     x_copy(7).start()
     stage_free(0)
-    term_other(6, 0, 0, 0)
-    hidden_block(7, 0, 1)
-    term_own(0, 0, 0)
+    term_other(6, own_rows(0), 0)
+    hidden_block(7, own_rows(1))
+    term_own(own_rows(0), 0)
     stage_free(1)
-    term_other(7, 0, 1, 1)
-    term_own(0, 1, 1)
+    term_other(7, own_rows(1), 1)
+    term_own(own_rows(1), 1)
 
     @pl.loop(0, 4)
     def _(t):
@@ -248,14 +255,13 @@
         peers[-1].start()
 
     def own_block(i):
-        for q in range(PIECES):
-            term_copy(6 + i, 0, i, i, q).wait_recv()
         for p in range(2):
             for q in range(PIECES):
-                total = summed(0, i, p, q, i)
+                total = summed(6 + i, own_rows(i), i, q, p)
                 for side in range(2):
-                    near_copy(0, i, p, q, side, 0).wait_recv()
-                    total += near[side, i, p, q].astype(jnp.float32)
+                    k = p if side == 1 else 1 - p
+                    near_copy(i, k, side, q).wait_recv()
+                    total += near[side, i, k, q].astype(jnp.float32)
                 dx[pl.ds(row_at(0, i, p), PART), cols_of(core, q)] = total.astype(dx.dtype)
             direct(i, p, p).start()
         direct(i, 1, 0).start()
@@ -304,8 +310,8 @@
         for p in range(2):
             for q in range(PIECES):
                 far_copy(i, p, q).wait_send()
-                for side in range(2):
-                    near_copy(2 * i + side, i, p, q, side, steps[side]).wait_send()
+                for k in range(2):
+                    near_copy(i, k, p, q).wait_send()
             for side in range(2):
                 direct(i, p, side).wait_send()
         for side in range(2):
@@ -361,9 +367,10 @@
                 pltpu.VMEM((2, 2, PIECES, PART, half // PIECES), bf16),
                 pltpu.VMEM((2, 2, 2, PIECES, PART, half // PIECES), bf16),
                 dma((3,)),
-                dma((4, 8)),
-                dma((2, PIECES)),
-                dma((8, PIECES)),
+                dma((3, 8, 2)),
+                dma((8,)),
+                dma((2, PIECES, 2)),
+                dma((8, PIECES, 2)),
                 dma((6, 2, PIECES)),
                 dma((2, 2, PIECES)),
                 dma((2, 2, 2, PIECES)),

time: 93.1 us -> 94.9 us (1.019)
  Pallas kernels: 92.2 us -> 94 us
    pallas_call x1, Pallas kernels: 86.4 us -> 88.1 us  [step(): pl.pallas_call(main_kernel, name='block_grads', out_shape=(pltpu.VMEM((to...]
where the time goes in v4:
time: 94.9 us; the launch traced here: 94.8 us
  Pallas kernels  94 us (99%)
    pallas_call x1, Pallas kernels, step(): pl.pallas_call(main_kernel, name='block_grads', out_shape=(pltpu.VMEM((to...  88.1 us
    pallas_call x1, Pallas kernels, step(): pl.pallas_call(write_kernel, name='write_out', out_shape=tuple((jax.Shape...  5.87 us

profile of v4, /device:TPU:113, one launch (start us, length us, event | category | flops | bytes accessed | tf_op | source)
XLA Modules:
  0.0 94.8 jit_solution(16455568150280294334)
XLA Ops:
  0.6 88.1 %block_grads.1 = (bf16[2048,2048]{1,0:T(8,128)(2,1)S(1)}, bf16[2048,1280]{1,0:T(8,128)(2,1)S(1)}, bf16[640,2048]{1,0:T(8,128)(2,1)S(1)}) custom-call(bf16[2048,2048]{1,0:T(8,128)(2,1)} %x_hbm.1, bf16[2048,2048]{1,0:T(8,128)(2,1)} %dy_hbm.1, bf16[2048,640]{1,0:T(8,128)(2,1)} %gate_hbm.1, bf16[2048,640]{1,0:T(8,128)(2,1)} %up_hbm.1, bf16[2048,640]{1,0:T(8,128)(2,1)} %wg_hbm.1, ...), custom_call_target="tpu_custom_call" | custom-call | tf_op jit(solution)/shard_map/block_grads/pallas_call | solution.py:349
  88.7 5.9 %write_out.1 = (bf16[2048,2048]{1,0:T(8,128)(2,1)}, bf16[2048,640]{1,0:T(8,128)(2,1)}, bf16[2048,640]{1,0:T(8,128)(2,1)}, bf16[640,2048]{1,0:T(8,128)(2,1)}) custom-call(bf16[2048,2048]{1,0:T(8,128)(2,1)S(1)} %get-tuple-element.7.dx, bf16[2048,1280]{1,0:T(8,128)(2,1)S(1)} %get-tuple-element.8.dw, bf16[640,2048]{1,0:T(8,128)(2,1)S(1)} %get-tuple-element.9.dwd), custom_call_target="tpu_custom_call" | custom-call | tf_op jit(solution)/shard_map/write_out/pallas_call | solution.py:386

commit v5 on v3

--- a/solution.py
+++ b/solution.py
@@ -223,11 +223,6 @@
     term_other(7, 0, 1, 1)
     term_own(0, 1, 1)
 
-    @pl.loop(0, 4)
-    def _(t):
-        cols = pl.ds(pl.multiple_of(t * (d // 4), d // 4), d // 4)
-        dwd[:, cols] = dot(hid_t[...], dy[:, cols], (1, 0)).astype(dwd.dtype)
-
     def direct(i, p, side):
         r = pl.ds(row_at(0, i, p), PART)
         return remote(
@@ -262,6 +257,12 @@
         direct(i, 0, 1).start()
         share(0, i, 0, BLOCK)
 
+    def down_tiles(lo, hi):
+        @pl.loop(lo, hi)
+        def _(t):
+            cols = pl.ds(pl.multiple_of(t * (d // 4), d // 4), d // 4)
+            dwd[:, cols] = dot(hid_t[...], dy[:, cols], (1, 0)).astype(dwd.dtype)
+
     def weight_tiles(lo, hi):
         @pl.loop(lo, hi)
         def _(t):
@@ -287,14 +288,16 @@
                 share(2, i, side, SHARE, k)
 
     own_block(0)
+    own_block(1)
+    down_tiles(0, 4)
+    relay(0)
     for b in range(8):
         x_copy(b).wait()
-    weight_tiles(0, 5)
-    own_block(1)
+    weight_tiles(0, 2)
+    keep(0)
+    weight_tiles(2, 5)
+    relay(1)
     weight_tiles(5, d // TILE)
-    relay(0)
-    keep(0)
-    relay(1)
     keep(1)
     last(0)
     last(1)

time: 93.1 us -> 91.9 us (0.987)
  Pallas kernels: 92.2 us -> 91 us
    pallas_call x1, Pallas kernels: 86.4 us -> 85.1 us  [step(): pl.pallas_call(main_kernel, name='block_grads', out_shape=(pltpu.VMEM((to...]
where the time goes in v5:
time: 91.9 us; the launch traced here: 91.8 us
  Pallas kernels  91 us (99%)
    pallas_call x1, Pallas kernels, step(): pl.pallas_call(main_kernel, name='block_grads', out_shape=(pltpu.VMEM((to...  85.1 us
    pallas_call x1, Pallas kernels, step(): pl.pallas_call(write_kernel, name='write_out', out_shape=tuple((jax.Shape...  5.87 us

profile of v5, /device:TPU:113, one launch (start us, length us, event | category | flops | bytes accessed | tf_op | source)
XLA Modules:
  0.0 91.8 jit_solution(4117179866615778231)
XLA Ops:
  0.6 85.1 %block_grads.1 = (bf16[2048,2048]{1,0:T(8,128)(2,1)S(1)}, bf16[2048,1280]{1,0:T(8,128)(2,1)S(1)}, bf16[640,2048]{1,0:T(8,128)(2,1)S(1)}) custom-call(bf16[2048,2048]{1,0:T(8,128)(2,1)} %x_hbm.1, bf16[2048,2048]{1,0:T(8,128)(2,1)} %dy_hbm.1, bf16[2048,640]{1,0:T(8,128)(2,1)} %gate_hbm.1, bf16[2048,640]{1,0:T(8,128)(2,1)} %up_hbm.1, bf16[2048,640]{1,0:T(8,128)(2,1)} %wg_hbm.1, ...), custom_call_target="tpu_custom_call" | custom-call | tf_op jit(solution)/shard_map/block_grads/pallas_call | solution.py:346
  85.8 5.9 %write_out.1 = (bf16[2048,2048]{1,0:T(8,128)(2,1)}, bf16[2048,640]{1,0:T(8,128)(2,1)}, bf16[2048,640]{1,0:T(8,128)(2,1)}, bf16[640,2048]{1,0:T(8,128)(2,1)}) custom-call(bf16[2048,2048]{1,0:T(8,128)(2,1)S(1)} %get-tuple-element.7.dx, bf16[2048,1280]{1,0:T(8,128)(2,1)S(1)} %get-tuple-element.8.dw, bf16[640,2048]{1,0:T(8,128)(2,1)S(1)} %get-tuple-element.9.dwd), custom_call_target="tpu_custom_call" | custom-call | tf_op jit(solution)/shard_map/write_out/pallas_call | solution.py:382

commit v6 on v4

--- a/solution.py
+++ b/solution.py
@@ -62,28 +62,27 @@
     def row_at(step, i, p=0):
         return pl.multiple_of(chip_at(step) * chunk_rows + i * BLOCK + p * PART, PART)
 
-    def far_rows(i):
-        return row_at(2, i, 0), row_at(2, i, 1)
-
-    def near_rows(i, k):
-        return row_at(1, i, 1 - k), row_at(CHIPS - 1, i, k)
-
-    def own_rows(i):
-        return row_at(0, i, 0), row_at(0, i, 1)
-
-    def row_copies(b, rows):
+    def far_runs(i):
+        return ((row_at(2, i), BLOCK),)
+
+    def near_runs(i):
+        return ((row_at(1, i), BLOCK), (row_at(CHIPS - 1, i), BLOCK))
+
+    own_runs = ((row_at(0, 0), 2 * BLOCK),)
+
+    def row_copies(b, runs):
         copies = []
-        for p in range(2):
-            r = pl.ds(rows[p], PART)
+        for n, (start, rows) in enumerate(runs):
+            r = pl.ds(start, rows)
             copies += [
-                pltpu.make_async_copy(dy_hbm.at[r], dy.at[r], row_sem.at[0, b, p]),
-                pltpu.make_async_copy(gate_hbm.at[r], gu.at[r, pl.ds(0, f)], row_sem.at[1, b, p]),
-                pltpu.make_async_copy(up_hbm.at[r], gu.at[r, pl.ds(f, f)], row_sem.at[2, b, p]),
+                pltpu.make_async_copy(dy_hbm.at[r], dy.at[r], row_sem.at[0, b, n]),
+                pltpu.make_async_copy(gate_hbm.at[r], gu.at[r, pl.ds(0, f)], row_sem.at[1, b, n]),
+                pltpu.make_async_copy(up_hbm.at[r], gu.at[r, pl.ds(f, f)], row_sem.at[2, b, n]),
             ]
         return copies
 
-    def start_rows(b, rows):
-        for c in row_copies(b, rows):
+    def start_rows(b, runs):
+        for c in row_copies(b, runs):
             c.start()
 
     def x_copy(b):
@@ -94,62 +93,73 @@
     in_wg = pltpu.make_async_copy(wg_hbm, w.at[:, pl.ds(0, f)], in_sem.at[1])
     in_wu = pltpu.make_async_copy(wu_hbm, w.at[:, pl.ds(f, f)], in_sem.at[2])
     in_wd.start()
-    start_rows(0, far_rows(0))
+    start_rows(0, far_runs(0))
     in_wg.start()
     in_wu.start()
-    start_rows(1, far_rows(1))
-
-    def both(ref, rows):
-        return jnp.concatenate([ref[pl.ds(r, PART), :] for r in rows], axis=0)
-
-    def hidden_block(b, rows):
-        for c in row_copies(b, rows):
+    start_rows(1, far_runs(1))
+
+    def gathered(ref, runs):
+        parts = [ref[pl.ds(start, rows), :] for start, rows in runs]
+        return parts[0] if len(parts) == 1 else jnp.concatenate(parts, axis=0)
+
+    def offsets(runs):
+        return [sum(rows for _, rows in runs[:n]) for n in range(len(runs))]
+
+    def hidden_block(b, runs):
+        for c in row_copies(b, runs):
             c.wait()
-        dh[...] = dot(both(dy, rows), wd[...], (1, 1))
-        for p in range(2):
-
-            @pl.loop(0, PART // STRIP)
+        dh[: sum(rows for _, rows in runs), :] = dot(gathered(dy, runs), wd[...], (1, 1))
+        for at, (start, rows) in zip(offsets(runs), runs):
+
+            @pl.loop(0, rows // STRIP)
             def _(s):
-                here = pl.ds(pl.multiple_of(p * PART + s * STRIP, STRIP), STRIP)
-                r = pl.ds(pl.multiple_of(rows[p] + s * STRIP, STRIP), STRIP)
+                here = pl.ds(pl.multiple_of(at + s * STRIP, STRIP), STRIP)
+                r = pl.ds(pl.multiple_of(start + s * STRIP, STRIP), STRIP)
                 h, back = jax.vjp(act, gu[r, pl.ds(0, f)].astype(jnp.float32), gu[r, pl.ds(f, f)].astype(jnp.float32))
                 d_gate, d_up = back(dh[here, :])
                 gu[r, pl.ds(0, f)] = d_gate.astype(gu.dtype)
                 gu[r, pl.ds(f, f)] = d_up.astype(gu.dtype)
                 hid[here, :] = h.astype(hid.dtype)
 
-            hid_t[:, pl.ds(rows[p], PART)] = hid[p * PART : (p + 1) * PART, :].T
+    def turn_hidden(runs):
+        for at, (start, rows) in zip(offsets(runs), runs):
+            hid_t[:, pl.ds(pl.multiple_of(start, BLOCK), rows)] = hid[at : at + rows, :].T
 
     def cols_of(c, q):
         return pl.ds(pl.multiple_of(c * half + q * width, width), width)
 
-    def term_copy(b, rows, slot, q, p):
-        return remote(
-            stage.at[slot, q, pl.ds(p * PART, PART)],
-            dx.at[pl.ds(rows[p], PART), cols_of(1 - core, q)],
-            term_send.at[slot, q, p],
-            term_recv.at[b, q, p],
-            peer,
-        )
-
-    def term_other(b, rows, slot):
+    def term_copies(b, runs, q):
+        return [
+            remote(
+                stage.at[q, pl.ds(at, rows)],
+                dx.at[pl.ds(start, rows), cols_of(1 - core, q)],
+                term_send.at[b, q, n],
+                term_recv.at[b, q, n],
+                peer,
+            )
+            for n, (at, (start, rows)) in enumerate(zip(offsets(runs), runs))
+        ]
+
+    def stage_free(b, runs):
         for q in range(PIECES):
-            stage[slot, q] = dot(both(gu, rows), w[cols_of(1 - core, q), :], (1, 1)).astype(stage.dtype)
-            for p in range(2):
-                term_copy(b, rows, slot, q, p).start()
-
-    def term_own(rows, slot):
+            for c in term_copies(b, runs, q):
+                c.wait_send()
+
+    def term_block(b, runs):
+        n = sum(rows for _, rows in runs)
         for q in range(PIECES):
-            own[slot, q] = dot(both(gu, rows), w[cols_of(core, q), :], (1, 1))
-
-    def stage_free(slot):
+            stage[q, :n] = dot(gathered(gu, runs), w[cols_of(1 - core, q), :], (1, 1)).astype(stage.dtype)
+            for c in term_copies(b, runs, q):
+                c.start()
         for q in range(PIECES):
-            for p in range(2):
-                term_copy(0, far_rows(0), slot, q, p).wait_send()
-
-    def summed(b, rows, slot, q, p):
-        term_copy(b, rows, slot, q, p).wait_recv()
-        return own[slot, q, p * PART : (p + 1) * PART, :] + dx[pl.ds(rows[p], PART), cols_of(core, q)].astype(jnp.float32)
+            own[q, :n] = dot(gathered(gu, runs), w[cols_of(core, q), :], (1, 1))
+
+    def term_arrived(b, runs, q):
+        for c in term_copies(b, runs, q):
+            c.wait_recv()
+
+    def summed(at, row, q):
+        return own[q, at : at + PART, :] + dx[pl.ds(row, PART), cols_of(core, q)].astype(jnp.float32)
 
     def far_copy(i, side, q):
         return remote(
@@ -170,70 +180,68 @@
             device_at(steps[side]),
         )
 
-    def finish_far(i):
-        for q in range(PIECES):
-            for side in range(2):
-                sendbuf[i, side, q] = summed(i, far_rows(i), i, q, side).astype(sendbuf.dtype)
-                far_copy(i, side, q).start()
-
     in_wd.wait()
-
-    hidden_block(0, far_rows(0))
-    start_rows(2, near_rows(0, 0))
-    x_copy(0).start()
-    in_wg.wait()
-    in_wu.wait()
-    pl.semaphore_wait(barrier, 3)
-    term_other(0, far_rows(0), 0)
-    term_own(far_rows(0), 0)
-    finish_far(0)
-
-    hidden_block(1, far_rows(1))
-    start_rows(3, near_rows(0, 1))
-    x_copy(1).start()
-    term_other(1, far_rows(1), 1)
-    hidden_block(2, near_rows(0, 0))
-    term_own(far_rows(1), 1)
-    finish_far(1)
 
     @pl.loop(0, 2)
     def _(i):
-        m = 1 - i
-        coming = (
-            (row_at(m, m, m), row_at(3 * m, m, 1 - m)),
-            (row_at(m, 1, 0), row_at(3 * m, 1, 1)),
-        )
+        runs = far_runs(i)
+        hidden_block(i, runs)
+        start_rows(2 + i, near_runs(i))
+        x_copy(i).start()
+
+        @pl.when(i == 0)
+        def _():
+            in_wg.wait()
+            in_wu.wait()
+            pl.semaphore_wait(barrier, 3)
+
+        @pl.when(i == 1)
+        def _():
+            stage_free(0, far_runs(0))
+
+        term_block(i, runs)
+        turn_hidden(runs)
+        for q in range(PIECES):
+            term_arrived(i, runs, q)
+            for side in range(2):
+                sendbuf[i, side, q] = summed(side * PART, row_at(2, i, side), q).astype(sendbuf.dtype)
+                far_copy(i, side, q).start()
+
+    stage_free(1, far_runs(1))
+    start_rows(4, own_runs)
+
+    @pl.loop(0, 2)
+    def _(i):
+        runs = near_runs(i)
+        hidden_block(2 + i, runs)
+        for n in range(2):
+            x_copy(2 + 2 * i + n).start()
+
+        @pl.when(i == 1)
+        def _():
+            stage_free(2, near_runs(0))
+
+        term_block(2 + i, runs)
+        turn_hidden(runs)
         for k in range(2):
-            b, rows = 2 + 2 * i + k, near_rows(i, k)
-            start_rows(b + 2, coming[k])
-            x_copy(b).start()
-            stage_free(k)
-            term_other(b, rows, k)
-            hidden_block(b + 1, near_rows(i, 1) if k == 0 else coming[0])
-            term_own(rows, k)
             for q in range(PIECES):
+                if k == 0:
+                    term_arrived(2 + i, runs, q)
                 for side in range(2):
-                    total = summed(b, rows, k, q, side)
+                    p = side if k == 1 else 1 - side
+                    total = summed(side * BLOCK + p * PART, row_at(steps[side], i, p), q)
                     if k == 1:
                         far_copy(i, side, q).wait_recv()
                         total += far[side, i, q].astype(jnp.float32)
-                    sendbuf[b, side, q] = total.astype(sendbuf.dtype)
+                    sendbuf[2 + 2 * i + k, side, q] = total.astype(sendbuf.dtype)
                     near_copy(i, k, side, q).start()
 
     x_copy(6).start()
     x_copy(7).start()
-    stage_free(0)
-    term_other(6, own_rows(0), 0)
-    hidden_block(7, own_rows(1))
-    term_own(own_rows(0), 0)
-    stage_free(1)
-    term_other(7, own_rows(1), 1)
-    term_own(own_rows(1), 1)
-
-    @pl.loop(0, 4)
-    def _(t):
-        cols = pl.ds(pl.multiple_of(t * (d // 4), d // 4), d // 4)
-        dwd[:, cols] = dot(hid_t[...], dy[:, cols], (1, 0)).astype(dwd.dtype)
+    hidden_block(4, own_runs)
+    stage_free(3, near_runs(1))
+    term_block(4, own_runs)
+    turn_hidden(own_runs)
 
     def direct(i, p, side):
         r = pl.ds(row_at(0, i, p), PART)
@@ -257,7 +265,7 @@
     def own_block(i):
         for p in range(2):
             for q in range(PIECES):
-                total = summed(6 + i, own_rows(i), i, q, p)
+                total = summed(i * BLOCK + p * PART, row_at(0, i, p), q)
                 for side in range(2):
                     k = p if side == 1 else 1 - p
                     near_copy(i, k, side, q).wait_recv()
@@ -268,6 +276,12 @@
         direct(i, 0, 1).start()
         share(0, i, 0, BLOCK)
 
+    def down_tiles(lo, hi):
+        @pl.loop(lo, hi)
+        def _(t):
+            cols = pl.ds(pl.multiple_of(t * (d // 4), d // 4), d // 4)
+            dwd[:, cols] = dot(hid_t[...], dy[:, cols], (1, 0)).astype(dwd.dtype)
+
     def weight_tiles(lo, hi):
         @pl.loop(lo, hi)
         def _(t):
@@ -292,29 +306,34 @@
                 forward(i, side, k).wait_recv()
                 share(2, i, side, SHARE, k)
 
+    down_tiles(0, 2)
+    for q in range(PIECES):
+        term_arrived(4, own_runs, q)
     own_block(0)
     for b in range(8):
         x_copy(b).wait()
-    weight_tiles(0, 5)
+    down_tiles(2, 4)
+    weight_tiles(0, 2)
     own_block(1)
-    weight_tiles(5, d // TILE)
+    weight_tiles(2, 4)
     relay(0)
+    weight_tiles(4, 6)
     keep(0)
+    weight_tiles(6, d // TILE)
     relay(1)
     keep(1)
     last(0)
     last(1)
 
+    stage_free(4, own_runs)
     for i in range(2):
-        stage_free(i)
-        for p in range(2):
+        for side in range(2):
             for q in range(PIECES):
-                far_copy(i, p, q).wait_send()
+                far_copy(i, side, q).wait_send()
                 for k in range(2):
-                    near_copy(i, k, p, q).wait_send()
-            for side in range(2):
+                    near_copy(i, k, side, q).wait_send()
+            for p in range(2):
                 direct(i, p, side).wait_send()
-        for side in range(2):
             for k in range(PART // SHARE):
                 forward(i, side, k).wait_send()
     for c in peers:
@@ -358,19 +377,19 @@
                 pltpu.VMEM((tokens, 2 * f), bf16),
                 pltpu.VMEM((d, 2 * f), bf16),
                 pltpu.VMEM((f, d), bf16),
-                pltpu.VMEM((BLOCK, f), bf16),
+                pltpu.VMEM((2 * BLOCK, f), bf16),
                 pltpu.VMEM((f, tokens), bf16),
-                pltpu.VMEM((BLOCK, f), f32),
-                pltpu.VMEM((2, PIECES, BLOCK, half // PIECES), f32),
-                pltpu.VMEM((2, PIECES, BLOCK, half // PIECES), bf16),
+                pltpu.VMEM((2 * BLOCK, f), f32),
+                pltpu.VMEM((PIECES, 2 * BLOCK, half // PIECES), f32),
+                pltpu.VMEM((PIECES, 2 * BLOCK, half // PIECES), bf16),
                 pltpu.VMEM((6, 2, PIECES, PART, half // PIECES), bf16),
                 pltpu.VMEM((2, 2, PIECES, PART, half // PIECES), bf16),
                 pltpu.VMEM((2, 2, 2, PIECES, PART, half // PIECES), bf16),
                 dma((3,)),
-                dma((3, 8, 2)),
+                dma((3, 5, 2)),
                 dma((8,)),
-                dma((2, PIECES, 2)),
-                dma((8, PIECES, 2)),
+                dma((5, PIECES, 2)),
+                dma((5, PIECES, 2)),
                 dma((6, 2, PIECES)),
                 dma((2, 2, PIECES)),
                 dma((2, 2, 2, PIECES)),

time: 94.9 us -> 91.1 us (0.960)
  Pallas kernels: 94 us -> 90.3 us
    pallas_call x1, Pallas kernels: 88.1 us -> 84.4 us  [step(): pl.pallas_call(main_kernel, name='block_grads', out_shape=(pltpu.VMEM((to...]
where the time goes in v6:
time: 91.1 us
  Pallas kernels  90.3 us (99%)
    pallas_call x1, Pallas kernels, step(): pl.pallas_call(main_kernel, name='block_grads', out_shape=(pltpu.VMEM((to...  84.4 us
    pallas_call x1, Pallas kernels, step(): pl.pallas_call(write_kernel, name='write_out', out_shape=tuple((jax.Shape...  5.87 us

profile of v6, /device:TPU:113, one launch (start us, length us, event | category | flops | bytes accessed | tf_op | source)
XLA Modules:
  0.0 91.1 jit_solution(12793856744079083303)
XLA Ops:
  0.6 84.4 %block_grads.1 = (bf16[2048,2048]{1,0:T(8,128)(2,1)S(1)}, bf16[2048,1280]{1,0:T(8,128)(2,1)S(1)}, bf16[640,2048]{1,0:T(8,128)(2,1)S(1)}) custom-call(bf16[2048,2048]{1,0:T(8,128)(2,1)} %x_hbm.1, bf16[2048,2048]{1,0:T(8,128)(2,1)} %dy_hbm.1, bf16[2048,640]{1,0:T(8,128)(2,1)} %gate_hbm.1, bf16[2048,640]{1,0:T(8,128)(2,1)} %up_hbm.1, bf16[2048,640]{1,0:T(8,128)(2,1)} %wg_hbm.1, ...), custom_call_target="tpu_custom_call" | custom-call | tf_op jit(solution)/shard_map/block_grads/pallas_call | solution.py:368
  85.0 5.9 %write_out.1 = (bf16[2048,2048]{1,0:T(8,128)(2,1)}, bf16[2048,640]{1,0:T(8,128)(2,1)}, bf16[2048,640]{1,0:T(8,128)(2,1)}, bf16[640,2048]{1,0:T(8,128)(2,1)}) custom-call(bf16[2048,2048]{1,0:T(8,128)(2,1)S(1)} %get-tuple-element.7.dx, bf16[2048,1280]{1,0:T(8,128)(2,1)S(1)} %get-tuple-element.8.dw, bf16[640,2048]{1,0:T(8,128)(2,1)S(1)} %get-tuple-element.9.dwd), custom_call_target="tpu_custom_call" | custom-call | tf_op jit(solution)/shard_map/write_out/pallas_call | solution.py:405

commit v7 on v6

--- a/solution.py
+++ b/solution.py
@@ -12,6 +12,7 @@
 BLOCK = 256
 PART = BLOCK // 2
 PIECES = 2
+NARROW = 256
 SHARE = 32
 STRIP = 32
 TILE = 256
@@ -29,8 +30,8 @@
     x_hbm, dy_hbm, gate_hbm, up_hbm, wg_hbm, wu_hbm, wd_hbm,
     dx, dw, dwd,
     x, dy, gu, w, wd, hid, hid_t, dh, own, stage, sendbuf, far, near,
-    in_sem, row_sem, x_sem, term_send, term_recv, rs_send, far_recv, near_recv,
-    ag_send, ag_recv, fwd_send, fwd_recv, peer_send, peer_recv,
+    first_sem, row_sem, x_sem, term_send, term_recv, rs_send, far_recv, near_recv,
+    ag_send, ag_recv, fwd_send, fwd_recv, peer_send, peer_recv, first_send, first_recv,
 ):
     tokens, d = x.shape
     f = wd.shape[0]
@@ -89,13 +90,30 @@
         r = pl.ds(pl.multiple_of(b * BLOCK, BLOCK), BLOCK)
         return pltpu.make_async_copy(x_hbm.at[r], x.at[r], x_sem.at[b])
 
-    in_wd = pltpu.make_async_copy(wd_hbm, wd, in_sem.at[0])
-    in_wg = pltpu.make_async_copy(wg_hbm, w.at[:, pl.ds(0, f)], in_sem.at[1])
-    in_wu = pltpu.make_async_copy(wu_hbm, w.at[:, pl.ds(f, f)], in_sem.at[2])
-    in_wd.start()
-    start_rows(0, far_runs(0))
-    in_wg.start()
-    in_wu.start()
+    first_rows = pl.ds(row_at(2, 0), BLOCK)
+
+    def first_copies(h):
+        cols = pl.ds(h * half, half)
+        return (
+            pltpu.make_async_copy(dy_hbm.at[first_rows, cols], dy.at[first_rows, cols], first_sem.at[0, h]),
+            pltpu.make_async_copy(wd_hbm.at[:, cols], wd.at[:, cols], first_sem.at[1, h]),
+        )
+
+    def w_copies(n, c):
+        r = pl.ds(pl.multiple_of(c * half, half), half)
+        return (
+            pltpu.make_async_copy(wg_hbm.at[r], w.at[r, pl.ds(0, f)], first_sem.at[2, n]),
+            pltpu.make_async_copy(wu_hbm.at[r], w.at[r, pl.ds(f, f)], first_sem.at[3, n]),
+        )
+
+    for h in range(2):
+        for c in first_copies(h):
+            c.start()
+    for c in row_copies(0, far_runs(0))[1:]:
+        c.start()
+    for n, c in enumerate((1 - core, core)):
+        for each in w_copies(n, c):
+            each.start()
     start_rows(1, far_runs(1))
 
     def gathered(ref, runs):
@@ -109,6 +127,9 @@
         for c in row_copies(b, runs):
             c.wait()
         dh[: sum(rows for _, rows in runs), :] = dot(gathered(dy, runs), wd[...], (1, 1))
+        through_act(runs)
+
+    def through_act(runs):
         for at, (start, rows) in zip(offsets(runs), runs):
 
             @pl.loop(0, rows // STRIP)
@@ -180,32 +201,70 @@
             device_at(steps[side]),
         )
 
-    in_wd.wait()
-
-    @pl.loop(0, 2)
-    def _(i):
-        runs = far_runs(i)
-        hidden_block(i, runs)
-        start_rows(2 + i, near_runs(i))
-        x_copy(i).start()
-
-        @pl.when(i == 0)
-        def _():
-            in_wg.wait()
-            in_wu.wait()
-            pl.semaphore_wait(barrier, 3)
-
-        @pl.when(i == 1)
-        def _():
-            stage_free(0, far_runs(0))
-
-        term_block(i, runs)
-        turn_hidden(runs)
-        for q in range(PIECES):
-            term_arrived(i, runs, q)
-            for side in range(2):
-                sendbuf[i, side, q] = summed(side * PART, row_at(2, i, side), q).astype(sendbuf.dtype)
-                far_copy(i, side, q).start()
+    def first_term(v):
+        cols = pl.ds(pl.multiple_of((1 - core) * half + v * NARROW, NARROW), NARROW)
+        q, here = v * NARROW // width, pl.ds(v * NARROW % width, NARROW)
+        return remote(
+            stage.at[q, pl.ds(0, BLOCK), here],
+            dx.at[first_rows, cols],
+            first_send.at[v],
+            first_recv.at[v],
+            peer,
+        )
+
+    def first_part(v, side):
+        q, here = v * NARROW // width, pl.ds(v * NARROW % width, NARROW)
+        return remote(
+            sendbuf.at[0, side, q, :, here],
+            far.at[side, 0, q, :, here],
+            rs_send.at[0, side, q],
+            far_recv.at[side, 0, q],
+            device_at(steps[side]),
+        )
+
+    for h in range(2):
+        for c in first_copies(h):
+            c.wait()
+        part = dot(dy[first_rows, h * half : (h + 1) * half], wd[:, h * half : (h + 1) * half], (1, 1))
+        dh[:BLOCK, :] = part if h == 0 else dh[:BLOCK, :] + part
+    for c in row_copies(0, far_runs(0))[1:]:
+        c.wait()
+    through_act(far_runs(0))
+    for c in w_copies(0, 1 - core):
+        c.wait()
+    pl.semaphore_wait(barrier, 3)
+    for v in range(half // NARROW):
+        q, here = v * NARROW // width, slice(v * NARROW % width, v * NARROW % width + NARROW)
+        cols = pl.ds(pl.multiple_of((1 - core) * half + v * NARROW, NARROW), NARROW)
+        stage[q, :BLOCK, here] = dot(gu[first_rows, :], w[cols, :], (1, 1)).astype(stage.dtype)
+        first_term(v).start()
+    for c in w_copies(1, core):
+        c.wait()
+    for v in range(half // NARROW):
+        q, here = v * NARROW // width, slice(v * NARROW % width, v * NARROW % width + NARROW)
+        cols = pl.ds(pl.multiple_of(core * half + v * NARROW, NARROW), NARROW)
+        total = dot(gu[first_rows, :], w[cols, :], (1, 1))
+        first_term(v).wait_recv()
+        total += dx[first_rows, cols].astype(jnp.float32)
+        for side in range(2):
+            sendbuf[0, side, q, :, here] = total[side * PART : (side + 1) * PART].astype(sendbuf.dtype)
+            first_part(v, side).start()
+    turn_hidden(far_runs(0))
+    start_rows(2, near_runs(0))
+    x_copy(0).start()
+
+    hidden_block(1, far_runs(1))
+    start_rows(3, near_runs(1))
+    x_copy(1).start()
+    for v in range(half // NARROW):
+        first_term(v).wait_send()
+    term_block(1, far_runs(1))
+    turn_hidden(far_runs(1))
+    for q in range(PIECES):
+        term_arrived(1, far_runs(1), q)
+        for side in range(2):
+            sendbuf[1, side, q] = summed(side * PART, row_at(2, 1, side), q).astype(sendbuf.dtype)
+            far_copy(1, side, q).start()
 
     stage_free(1, far_runs(1))
     start_rows(4, own_runs)
@@ -385,7 +444,7 @@
                 pltpu.VMEM((6, 2, PIECES, PART, half // PIECES), bf16),
                 pltpu.VMEM((2, 2, PIECES, PART, half // PIECES), bf16),
                 pltpu.VMEM((2, 2, 2, PIECES, PART, half // PIECES), bf16),
-                dma((3,)),
+                dma((4, 2)),
                 dma((3, 5, 2)),
                 dma((8,)),
                 dma((5, PIECES, 2)),
@@ -399,6 +458,8 @@
                 dma((2, 2, PART // SHARE)),
                 dma((10 + 4 * PART // SHARE,)),
                 dma((10 + 4 * PART // SHARE,)),
+                dma((half // NARROW,)),
+                dma((half // NARROW,)),
             ],
             compiler_params=pltpu.CompilerParams(collective_id=0, has_side_effects=True, vmem_limit_bytes=47 * 2**20),
         )(x, dy, gate, up, w_gate, w_up, w_down)

time: 91.1 us -> 92.7 us (1.018)
  Pallas kernels: 90.3 us -> 91.8 us
    pallas_call x1, Pallas kernels: 84.4 us -> 85.9 us  [step(): pl.pallas_call(main_kernel, name='block_grads', out_shape=(pltpu.VMEM((to...]
where the time goes in v7:
time: 92.7 us; the launch traced here: 92.6 us
  Pallas kernels  91.8 us (99%)
    pallas_call x1, Pallas kernels, step(): pl.pallas_call(main_kernel, name='block_grads', out_shape=(pltpu.VMEM((to...  85.9 us
    pallas_call x1, Pallas kernels, step(): pl.pallas_call(write_kernel, name='write_out', out_shape=tuple((jax.Shape...  5.87 us

profile of v7, /device:TPU:113, one launch (start us, length us, event | category | flops | bytes accessed | tf_op | source)
XLA Modules:
  0.0 92.6 jit_solution(10391418225097560307)
XLA Ops:
  0.6 85.9 %block_grads.1 = (bf16[2048,2048]{1,0:T(8,128)(2,1)S(1)}, bf16[2048,1280]{1,0:T(8,128)(2,1)S(1)}, bf16[640,2048]{1,0:T(8,128)(2,1)S(1)}) custom-call(bf16[2048,2048]{1,0:T(8,128)(2,1)} %x_hbm.1, bf16[2048,2048]{1,0:T(8,128)(2,1)} %dy_hbm.1, bf16[2048,640]{1,0:T(8,128)(2,1)} %gate_hbm.1, bf16[2048,640]{1,0:T(8,128)(2,1)} %up_hbm.1, bf16[2048,640]{1,0:T(8,128)(2,1)} %wg_hbm.1, ...), custom_call_target="tpu_custom_call" | custom-call | tf_op jit(solution)/shard_map/block_grads/pallas_call | solution.py:427
  86.6 5.9 %write_out.1 = (bf16[2048,2048]{1,0:T(8,128)(2,1)}, bf16[2048,640]{1,0:T(8,128)(2,1)}, bf16[2048,640]{1,0:T(8,128)(2,1)}, bf16[640,2048]{1,0:T(8,128)(2,1)}) custom-call(bf16[2048,2048]{1,0:T(8,128)(2,1)S(1)} %get-tuple-element.7.dx, bf16[2048,1280]{1,0:T(8,128)(2,1)S(1)} %get-tuple-element.8.dw, bf16[640,2048]{1,0:T(8,128)(2,1)S(1)} %get-tuple-element.9.dwd), custom_call_target="tpu_custom_call" | custom-call | tf_op jit(solution)/shard_map/write_out/pallas_call | solution.py:466

commit v8 on v7

--- a/solution.py
+++ b/solution.py
@@ -12,7 +12,6 @@
 BLOCK = 256
 PART = BLOCK // 2
 PIECES = 2
-NARROW = 256
 SHARE = 32
 STRIP = 32
 TILE = 256
@@ -170,6 +169,7 @@
         n = sum(rows for _, rows in runs)
         for q in range(PIECES):
             stage[q, :n] = dot(gathered(gu, runs), w[cols_of(1 - core, q), :], (1, 1)).astype(stage.dtype)
+        for q in range(PIECES):
             for c in term_copies(b, runs, q):
                 c.start()
         for q in range(PIECES):
@@ -202,24 +202,12 @@
         )
 
     def first_term(v):
-        cols = pl.ds(pl.multiple_of((1 - core) * half + v * NARROW, NARROW), NARROW)
-        q, here = v * NARROW // width, pl.ds(v * NARROW % width, NARROW)
         return remote(
-            stage.at[q, pl.ds(0, BLOCK), here],
-            dx.at[first_rows, cols],
+            stage.at[v, pl.ds(0, BLOCK)],
+            dx.at[first_rows, cols_of(1 - core, v)],
             first_send.at[v],
             first_recv.at[v],
             peer,
-        )
-
-    def first_part(v, side):
-        q, here = v * NARROW // width, pl.ds(v * NARROW % width, NARROW)
-        return remote(
-            sendbuf.at[0, side, q, :, here],
-            far.at[side, 0, q, :, here],
-            rs_send.at[0, side, q],
-            far_recv.at[side, 0, q],
-            device_at(steps[side]),
         )
 
     for h in range(2):
@@ -233,22 +221,18 @@
     for c in w_copies(0, 1 - core):
         c.wait()
     pl.semaphore_wait(barrier, 3)
-    for v in range(half // NARROW):
-        q, here = v * NARROW // width, slice(v * NARROW % width, v * NARROW % width + NARROW)
-        cols = pl.ds(pl.multiple_of((1 - core) * half + v * NARROW, NARROW), NARROW)
-        stage[q, :BLOCK, here] = dot(gu[first_rows, :], w[cols, :], (1, 1)).astype(stage.dtype)
+    for v in range(PIECES):
+        stage[v, :BLOCK] = dot(gu[first_rows, :], w[cols_of(1 - core, v), :], (1, 1)).astype(stage.dtype)
         first_term(v).start()
     for c in w_copies(1, core):
         c.wait()
-    for v in range(half // NARROW):
-        q, here = v * NARROW // width, slice(v * NARROW % width, v * NARROW % width + NARROW)
-        cols = pl.ds(pl.multiple_of(core * half + v * NARROW, NARROW), NARROW)
-        total = dot(gu[first_rows, :], w[cols, :], (1, 1))
+    for q in range(PIECES):
+        own[q, :BLOCK] = dot(gu[first_rows, :], w[cols_of(core, q), :], (1, 1))
+    for v in range(PIECES):
         first_term(v).wait_recv()
-        total += dx[first_rows, cols].astype(jnp.float32)
         for side in range(2):
-            sendbuf[0, side, q, :, here] = total[side * PART : (side + 1) * PART].astype(sendbuf.dtype)
-            first_part(v, side).start()
+            sendbuf[0, side, v] = summed(side * PART, row_at(2, 0, side), v).astype(sendbuf.dtype)
+            far_copy(0, side, v).start()
     turn_hidden(far_runs(0))
     start_rows(2, near_runs(0))
     x_copy(0).start()
@@ -256,7 +240,7 @@
     hidden_block(1, far_runs(1))
     start_rows(3, near_runs(1))
     x_copy(1).start()
-    for v in range(half // NARROW):
+    for v in range(PIECES):
         first_term(v).wait_send()
     term_block(1, far_runs(1))
     turn_hidden(far_runs(1))
@@ -381,8 +365,6 @@
     weight_tiles(6, d // TILE)
     relay(1)
     keep(1)
-    last(0)
-    last(1)
 
     stage_free(4, own_runs)
     for i in range(2):
@@ -393,9 +375,18 @@
                     near_copy(i, k, side, q).wait_send()
             for p in range(2):
                 direct(i, p, side).wait_send()
-            for k in range(PART // SHARE):
-                forward(i, side, k).wait_send()
+    done = len(peers)
     for c in peers:
+        c.wait()
+    last(0)
+    for side in range(2):
+        for k in range(PART // SHARE):
+            forward(0, side, k).wait_send()
+    last(1)
+    for side in range(2):
+        for k in range(PART // SHARE):
+            forward(1, side, k).wait_send()
+    for c in peers[done:]:
         c.wait()
 
 
@@ -458,8 +449,8 @@
                 dma((2, 2, PART // SHARE)),
                 dma((10 + 4 * PART // SHARE,)),
                 dma((10 + 4 * PART // SHARE,)),
-                dma((half // NARROW,)),
-                dma((half // NARROW,)),
+                dma((PIECES,)),
+                dma((PIECES,)),
             ],
             compiler_params=pltpu.CompilerParams(collective_id=0, has_side_effects=True, vmem_limit_bytes=47 * 2**20),
         )(x, dy, gate, up, w_gate, w_up, w_down)

time: 92.7 us -> 90.8 us (0.980)
  Pallas kernels: 91.8 us -> 90 us
    pallas_call x1, Pallas kernels: 85.9 us -> 84.1 us  [step(): pl.pallas_call(main_kernel, name='block_grads', out_shape=(pltpu.VMEM((to...]
where the time goes in v8:
time: 90.8 us
  Pallas kernels  90 us (99%)
    pallas_call x1, Pallas kernels, step(): pl.pallas_call(main_kernel, name='block_grads', out_shape=(pltpu.VMEM((to...  84.1 us
    pallas_call x1, Pallas kernels, step(): pl.pallas_call(write_kernel, name='write_out', out_shape=tuple((jax.Shape...  5.87 us

profile of v8, /device:TPU:113, one launch (start us, length us, event | category | flops | bytes accessed | tf_op | source)
XLA Modules:
  0.0 90.8 jit_solution(18365031804958391648)
XLA Ops:
  0.6 84.1 %block_grads.1 = (bf16[2048,2048]{1,0:T(8,128)(2,1)S(1)}, bf16[2048,1280]{1,0:T(8,128)(2,1)S(1)}, bf16[640,2048]{1,0:T(8,128)(2,1)S(1)}) custom-call(bf16[2048,2048]{1,0:T(8,128)(2,1)} %x_hbm.1, bf16[2048,2048]{1,0:T(8,128)(2,1)} %dy_hbm.1, bf16[2048,640]{1,0:T(8,128)(2,1)} %gate_hbm.1, bf16[2048,640]{1,0:T(8,128)(2,1)} %up_hbm.1, bf16[2048,640]{1,0:T(8,128)(2,1)} %wg_hbm.1, ...), custom_call_target="tpu_custom_call" | custom-call | tf_op jit(solution)/shard_map/block_grads/pallas_call | solution.py:418
  84.7 5.9 %write_out.1 = (bf16[2048,2048]{1,0:T(8,128)(2,1)}, bf16[2048,640]{1,0:T(8,128)(2,1)}, bf16[2048,640]{1,0:T(8,128)(2,1)}, bf16[640,2048]{1,0:T(8,128)(2,1)}) custom-call(bf16[2048,2048]{1,0:T(8,128)(2,1)S(1)} %get-tuple-element.7.dx, bf16[2048,1280]{1,0:T(8,128)(2,1)S(1)} %get-tuple-element.8.dw, bf16[640,2048]{1,0:T(8,128)(2,1)S(1)} %get-tuple-element.9.dwd), custom_call_target="tpu_custom_call" | custom-call | tf_op jit(solution)/shard_map/write_out/pallas_call | solution.py:457

commit v9 on v8

--- a/solution.py
+++ b/solution.py
@@ -68,6 +68,9 @@
     def near_runs(i):
         return ((row_at(1, i), BLOCK), (row_at(CHIPS - 1, i), BLOCK))
 
+    def sent_runs(i, k):
+        return ((row_at(1, i, 1 - k), PART), (row_at(CHIPS - 1, i, k), PART))
+
     own_runs = ((row_at(0, 0), 2 * BLOCK),)
 
     def row_copies(b, runs):
@@ -148,10 +151,10 @@
     def cols_of(c, q):
         return pl.ds(pl.multiple_of(c * half + q * width, width), width)
 
-    def term_copies(b, runs, q):
+    def term_copies(b, runs, q, base=0):
         return [
             remote(
-                stage.at[q, pl.ds(at, rows)],
+                stage.at[q, pl.ds(base + at, rows)],
                 dx.at[pl.ds(start, rows), cols_of(1 - core, q)],
                 term_send.at[b, q, n],
                 term_recv.at[b, q, n],
@@ -165,15 +168,14 @@
             for c in term_copies(b, runs, q):
                 c.wait_send()
 
-    def term_block(b, runs):
+    def term_block(b, runs, base=0):
         n = sum(rows for _, rows in runs)
         for q in range(PIECES):
-            stage[q, :n] = dot(gathered(gu, runs), w[cols_of(1 - core, q), :], (1, 1)).astype(stage.dtype)
-        for q in range(PIECES):
-            for c in term_copies(b, runs, q):
+            stage[q, base : base + n] = dot(gathered(gu, runs), w[cols_of(1 - core, q), :], (1, 1)).astype(stage.dtype)
+            for c in term_copies(b, runs, q, base):
                 c.start()
         for q in range(PIECES):
-            own[q, :n] = dot(gathered(gu, runs), w[cols_of(core, q), :], (1, 1))
+            own[q, base : base + n] = dot(gathered(gu, runs), w[cols_of(core, q), :], (1, 1))
 
     def term_arrived(b, runs, q):
         for c in term_copies(b, runs, q):
@@ -262,28 +264,30 @@
 
         @pl.when(i == 1)
         def _():
-            stage_free(2, near_runs(0))
-
-        term_block(2 + i, runs)
-        turn_hidden(runs)
+            for k in range(2):
+                stage_free(2 + k, sent_runs(0, k))
+
         for k in range(2):
+            b, sent = 2 + 2 * i + k, sent_runs(i, k)
+            term_block(b, sent, k * BLOCK)
+            if k == 0:
+                turn_hidden(runs)
             for q in range(PIECES):
-                if k == 0:
-                    term_arrived(2 + i, runs, q)
+                term_arrived(b, sent, q)
                 for side in range(2):
-                    p = side if k == 1 else 1 - side
-                    total = summed(side * BLOCK + p * PART, row_at(steps[side], i, p), q)
+                    total = summed(k * BLOCK + side * PART, sent[side][0], q)
                     if k == 1:
                         far_copy(i, side, q).wait_recv()
                         total += far[side, i, q].astype(jnp.float32)
-                    sendbuf[2 + 2 * i + k, side, q] = total.astype(sendbuf.dtype)
+                    sendbuf[b, side, q] = total.astype(sendbuf.dtype)
                     near_copy(i, k, side, q).start()
 
     x_copy(6).start()
     x_copy(7).start()
     hidden_block(4, own_runs)
-    stage_free(3, near_runs(1))
-    term_block(4, own_runs)
+    for k in range(2):
+        stage_free(4 + k, sent_runs(1, k))
+    term_block(6, own_runs)
     turn_hidden(own_runs)
 
     def direct(i, p, side):
@@ -351,7 +355,7 @@
 
     down_tiles(0, 2)
     for q in range(PIECES):
-        term_arrived(4, own_runs, q)
+        term_arrived(6, own_runs, q)
     own_block(0)
     for b in range(8):
         x_copy(b).wait()
@@ -366,7 +370,7 @@
     relay(1)
     keep(1)
 
-    stage_free(4, own_runs)
+    stage_free(6, own_runs)
     for i in range(2):
         for side in range(2):
             for q in range(PIECES):
@@ -438,8 +442,8 @@
                 dma((4, 2)),
                 dma((3, 5, 2)),
                 dma((8,)),
-                dma((5, PIECES, 2)),
-                dma((5, PIECES, 2)),
+                dma((7, PIECES, 2)),
+                dma((7, PIECES, 2)),
                 dma((6, 2, PIECES)),
                 dma((2, 2, PIECES)),
                 dma((2, 2, 2, PIECES)),

time: 90.8 us -> 90.6 us (level)
  no operation moved by 1% of the time
where the time goes in v9:
time: 90.6 us; the launch traced here: 90.5 us
  Pallas kernels  89.7 us (99%)
    pallas_call x1, Pallas kernels, step(): pl.pallas_call(main_kernel, name='block_grads', out_shape=(pltpu.VMEM((to...  83.8 us
    pallas_call x1, Pallas kernels, step(): pl.pallas_call(write_kernel, name='write_out', out_shape=tuple((jax.Shape...  5.87 us

profile of v9, /device:TPU:113, one launch (start us, length us, event | category | flops | bytes accessed | tf_op | source)
XLA Modules:
  0.0 90.5 jit_solution(14400808692011691220)
XLA Ops:
  0.6 83.8 %block_grads.1 = (bf16[2048,2048]{1,0:T(8,128)(2,1)S(1)}, bf16[2048,1280]{1,0:T(8,128)(2,1)S(1)}, bf16[640,2048]{1,0:T(8,128)(2,1)S(1)}) custom-call(bf16[2048,2048]{1,0:T(8,128)(2,1)} %x_hbm.1, bf16[2048,2048]{1,0:T(8,128)(2,1)} %dy_hbm.1, bf16[2048,640]{1,0:T(8,128)(2,1)} %gate_hbm.1, bf16[2048,640]{1,0:T(8,128)(2,1)} %up_hbm.1, bf16[2048,640]{1,0:T(8,128)(2,1)} %wg_hbm.1, ...), custom_call_target="tpu_custom_call" | custom-call | tf_op jit(solution)/shard_map/block_grads/pallas_call | solution.py:422
  84.5 5.9 %write_out.1 = (bf16[2048,2048]{1,0:T(8,128)(2,1)}, bf16[2048,640]{1,0:T(8,128)(2,1)}, bf16[2048,640]{1,0:T(8,128)(2,1)}, bf16[640,2048]{1,0:T(8,128)(2,1)}) custom-call(bf16[2048,2048]{1,0:T(8,128)(2,1)S(1)} %get-tuple-element.7.dx, bf16[2048,1280]{1,0:T(8,128)(2,1)S(1)} %get-tuple-element.8.dw, bf16[640,2048]{1,0:T(8,128)(2,1)S(1)} %get-tuple-element.9.dwd), custom_call_target="tpu_custom_call" | custom-call | tf_op jit(solution)/shard_map/write_out/pallas_call | solution.py:461

commit v10 on v9

--- a/solution.py
+++ b/solution.py
@@ -65,9 +65,6 @@
     def far_runs(i):
         return ((row_at(2, i), BLOCK),)
 
-    def near_runs(i):
-        return ((row_at(1, i), BLOCK), (row_at(CHIPS - 1, i), BLOCK))
-
     def sent_runs(i, k):
         return ((row_at(1, i, 1 - k), PART), (row_at(CHIPS - 1, i, k), PART))
 
@@ -146,7 +143,7 @@
 
     def turn_hidden(runs):
         for at, (start, rows) in zip(offsets(runs), runs):
-            hid_t[:, pl.ds(pl.multiple_of(start, BLOCK), rows)] = hid[at : at + rows, :].T
+            hid_t[:, pl.ds(pl.multiple_of(start, PART), rows)] = hid[at : at + rows, :].T
 
     def cols_of(c, q):
         return pl.ds(pl.multiple_of(c * half + q * width, width), width)
@@ -236,11 +233,13 @@
             sendbuf[0, side, v] = summed(side * PART, row_at(2, 0, side), v).astype(sendbuf.dtype)
             far_copy(0, side, v).start()
     turn_hidden(far_runs(0))
-    start_rows(2, near_runs(0))
+    for k in range(2):
+        start_rows(2 + k, sent_runs(0, k))
     x_copy(0).start()
 
     hidden_block(1, far_runs(1))
-    start_rows(3, near_runs(1))
+    for k in range(2):
+        start_rows(4 + k, sent_runs(1, k))
     x_copy(1).start()
     for v in range(PIECES):
         first_term(v).wait_send()
@@ -253,12 +252,10 @@
             far_copy(1, side, q).start()
 
     stage_free(1, far_runs(1))
-    start_rows(4, own_runs)
+    start_rows(6, own_runs)
 
     @pl.loop(0, 2)
     def _(i):
-        runs = near_runs(i)
-        hidden_block(2 + i, runs)
         for n in range(2):
             x_copy(2 + 2 * i + n).start()
 
@@ -269,9 +266,9 @@
 
         for k in range(2):
             b, sent = 2 + 2 * i + k, sent_runs(i, k)
+            hidden_block(b, sent)
             term_block(b, sent, k * BLOCK)
-            if k == 0:
-                turn_hidden(runs)
+            turn_hidden(sent)
             for q in range(PIECES):
                 term_arrived(b, sent, q)
                 for side in range(2):
@@ -284,7 +281,7 @@
 
     x_copy(6).start()
     x_copy(7).start()
-    hidden_block(4, own_runs)
+    hidden_block(6, own_runs)
     for k in range(2):
         stage_free(4 + k, sent_runs(1, k))
     term_block(6, own_runs)
@@ -353,18 +350,17 @@
                 forward(i, side, k).wait_recv()
                 share(2, i, side, SHARE, k)
 
-    down_tiles(0, 2)
     for q in range(PIECES):
         term_arrived(6, own_runs, q)
     own_block(0)
+    down_tiles(0, 4)
     for b in range(8):
         x_copy(b).wait()
-    down_tiles(2, 4)
-    weight_tiles(0, 2)
+    weight_tiles(0, 1)
     own_block(1)
-    weight_tiles(2, 4)
+    weight_tiles(1, 3)
     relay(0)
-    weight_tiles(4, 6)
+    weight_tiles(3, 6)
     keep(0)
     weight_tiles(6, d // TILE)
     relay(1)
@@ -440,7 +436,7 @@
                 pltpu.VMEM((2, 2, PIECES, PART, half // PIECES), bf16),
                 pltpu.VMEM((2, 2, 2, PIECES, PART, half // PIECES), bf16),
                 dma((4, 2)),
-                dma((3, 5, 2)),
+                dma((3, 7, 2)),
                 dma((8,)),
                 dma((7, PIECES, 2)),
                 dma((7, PIECES, 2)),

time: 90.6 us -> 89 us (0.982)
  Pallas kernels: 89.7 us -> 88.1 us
    pallas_call x1, Pallas kernels: 83.8 us -> 82.2 us  [step(): pl.pallas_call(main_kernel, name='block_grads', out_shape=(pltpu.VMEM((to...]
where the time goes in v10:
time: 89 us; the launch traced here: 88.9 us
  Pallas kernels  88.1 us (99%)
    pallas_call x1, Pallas kernels, step(): pl.pallas_call(main_kernel, name='block_grads', out_shape=(pltpu.VMEM((to...  82.2 us
    pallas_call x1, Pallas kernels, step(): pl.pallas_call(write_kernel, name='write_out', out_shape=tuple((jax.Shape...  5.87 us

profile of v10, /device:TPU:113, one launch (start us, length us, event | category | flops | bytes accessed | tf_op | source)
XLA Modules:
  0.0 88.9 jit_solution(12761866606844151064)
XLA Ops:
  0.6 82.2 %block_grads.1 = (bf16[2048,2048]{1,0:T(8,128)(2,1)S(1)}, bf16[2048,1280]{1,0:T(8,128)(2,1)S(1)}, bf16[640,2048]{1,0:T(8,128)(2,1)S(1)}) custom-call(bf16[2048,2048]{1,0:T(8,128)(2,1)} %x_hbm.1, bf16[2048,2048]{1,0:T(8,128)(2,1)} %dy_hbm.1, bf16[2048,640]{1,0:T(8,128)(2,1)} %gate_hbm.1, bf16[2048,640]{1,0:T(8,128)(2,1)} %up_hbm.1, bf16[2048,640]{1,0:T(8,128)(2,1)} %wg_hbm.1, ...), custom_call_target="tpu_custom_call" | custom-call | tf_op jit(solution)/shard_map/block_grads/pallas_call | solution.py:418
  82.9 5.9 %write_out.1 = (bf16[2048,2048]{1,0:T(8,128)(2,1)}, bf16[2048,640]{1,0:T(8,128)(2,1)}, bf16[2048,640]{1,0:T(8,128)(2,1)}, bf16[640,2048]{1,0:T(8,128)(2,1)}) custom-call(bf16[2048,2048]{1,0:T(8,128)(2,1)S(1)} %get-tuple-element.7.dx, bf16[2048,1280]{1,0:T(8,128)(2,1)S(1)} %get-tuple-element.8.dw, bf16[640,2048]{1,0:T(8,128)(2,1)S(1)} %get-tuple-element.9.dwd), custom_call_target="tpu_custom_call" | custom-call | tf_op jit(solution)/shard_map/write_out/pallas_call | solution.py:457
